TPU v7x, 32 devices: a whole 2x2x4 slice. The times are simulated.
32 devices in a mesh: groups: 2 (over x), steps: 8 (over z, y), inner: 2 (over core).
Axes of the slice: x: 2, y: 2, z: 4, core: 2. Of those that a mesh axis runs over, the one named last changes fastest.
Arguments:
- start_state: float32 [16, 32, 768], P('groups'), parts along dimension 0, may hold values from -6 to 6
- noise_draws: float32 [32, 8, 32, 768], P(('groups', 'steps', 'inner')), parts along dimension 0, may hold values from -6 to 6
- step_gaps: int32 [32], P(('groups', 'steps', 'inner')), parts along dimension 0, may hold values from 1 to 15
- window_start: int32 [2], P('groups'), parts along dimension 0, may hold values from 240 to 999
- input_weight: bfloat16 [768, 1024], replicated, may hold values from -0.21875 to 0.21875
- embed_weight: bfloat16 [256, 2048], replicated, may hold values from -0.375 to 0.375
- first_weight: bfloat16 [1024, 1024], replicated, may hold values from -0.1875 to 0.1875
- second_weight: bfloat16 [1024, 1024], replicated, may hold values from -0.1875 to 0.1875
- output_weight: bfloat16 [1024, 768], replicated, may hold values from -0.1875 to 0.1875
Outputs:
- trajectory: float32 [32, 8, 32, 768], P(('groups', 'steps', 'inner')), parts along dimension 0
There are 2 independent parts, one for each index of `groups`. A program takes and returns all parts, laid end to end along the dimension named above; an argument that names none is the same for every part. Nothing has to cross between parts.
All inputs are finite; a program needn't handle non-finite values.
Results may differ from a plain program's by a relative error of at most 0.00035.
Values sent between devices are 32-bit elements; how exact they have to be, the bound alone decides.
No kernel may reach another device: no remote copies, remote signals or barrier semaphores. Data moves between devices by JAX's collectives and lax.ppermute only.
A program may use at most 64 MiB of HBM per device.

v0:
```python
import math

import jax
import jax.numpy as jnp
from jax import lax
from jax.sharding import PartitionSpec as P

GROUPS = 32
ITERS = 2
TRAIN_STEPS = 1000


def prefix_2(part, axis, combine, identity):
    place = lax.axis_index(axis)
    gathered = lax.all_gather(part, axis)
    state = jnp.zeros_like(part) + jnp.asarray(identity, part.dtype)

    def one(turn, state):
        return combine(state, lax.dynamic_index_in_dim(gathered, turn, 0, False))

    return lax.fori_loop(0, place, one, state)


def noise_table():
    levels = jnp.arange(TRAIN_STEPS, dtype=jnp.float32)
    beta_values = 0.0001 + (0.02 - 0.0001) * levels / (TRAIN_STEPS - 1)
    return jnp.exp(jnp.cumsum(jnp.log1p(-beta_values)))


def lookup(table, noise_level):
    places = jnp.arange(TRAIN_STEPS, dtype=jnp.int32)
    return jnp.sum(jnp.where(places == noise_level, table, jnp.zeros_like(table)))


def group_norm(hidden, batch_count):
    total_rows, channel_count = hidden.shape
    shaped = hidden.reshape(batch_count, total_rows // batch_count, channel_count)

    def group_mean(values):
        per_channel = jnp.mean(values, axis=1).reshape(batch_count, GROUPS, channel_count // GROUPS)
        per_group = jnp.mean(per_channel, axis=2, keepdims=True)
        return jnp.broadcast_to(per_group, per_channel.shape).reshape(batch_count, 1, channel_count)

    center = group_mean(shaped)
    offset = shaped - center
    spread = group_mean(offset * offset)
    return (offset * lax.rsqrt(spread + 1e-05)).reshape(total_rows, channel_count)


def predict_noise(
    state, noise_level, input_weight, embed_weight, first_weight, second_weight, output_weight
):
    batch_count, patch_count, feature_count = state.shape
    channel_count = input_weight.shape[1]
    flat_state = state.reshape(batch_count * patch_count, feature_count).astype(jnp.bfloat16)
    entry_hidden = jnp.dot(flat_state, input_weight, preferred_element_type=jnp.float32)
    half_count = embed_weight.shape[0] // 2
    frequency = jnp.exp(-math.log(10000.0) * jnp.arange(half_count, dtype=jnp.float32) / half_count)
    angles = noise_level.astype(jnp.float32) * frequency
    features = jnp.concatenate([jnp.cos(angles), jnp.sin(angles)])[None, :].astype(jnp.bfloat16)
    modulation = jnp.dot(features, embed_weight, preferred_element_type=jnp.float32)
    scale_part = modulation[:, :channel_count]
    shift_part = modulation[:, channel_count:]
    act_one = jax.nn.silu(
        group_norm(entry_hidden, batch_count) * (1.0 + scale_part) + shift_part
    ).astype(jnp.bfloat16)
    middle = jnp.dot(act_one, first_weight, preferred_element_type=jnp.float32)
    act_two = jax.nn.silu(group_norm(middle, batch_count)).astype(jnp.bfloat16)
    block_out = entry_hidden + jnp.dot(act_two, second_weight, preferred_element_type=jnp.float32)
    act_three = jax.nn.silu(group_norm(block_out, batch_count)).astype(jnp.bfloat16)
    predicted = jnp.dot(act_three, output_weight, preferred_element_type=jnp.float32)
    return predicted.reshape(state.shape)


def drift_of(
    state,
    noise_draw,
    level_now,
    level_next,
    table,
    input_weight,
    embed_weight,
    first_weight,
    second_weight,
    output_weight,
):
    predicted = predict_noise(
        state, level_now, input_weight, embed_weight, first_weight, second_weight, output_weight
    )
    bar_now = lookup(table, level_now)
    bar_next = lookup(table, level_next)
    clean_guess = jnp.clip(
        (state - jnp.sqrt(1.0 - bar_now) * predicted) / jnp.sqrt(bar_now), -1.0, 1.0
    )
    implied = (state - jnp.sqrt(bar_now) * clean_guess) / jnp.sqrt(1.0 - bar_now)
    sigma_value = jnp.sqrt((1.0 - bar_next) / (1.0 - bar_now) * (1.0 - bar_now / bar_next))
    noise_coef = (1.0 - bar_next) * jnp.sqrt(bar_now / (bar_next * (1.0 - bar_now)))
    return (
        jnp.sqrt(bar_next) * clean_guess + noise_coef * implied + sigma_value * noise_draw - state
    )


def add_terms(earlier, later):
    return earlier + later


def shards(
    start_state,
    noise_draws,
    step_gaps,
    window_start,
    input_weight,
    embed_weight,
    first_weight,
    second_weight,
    output_weight,
):
    table = noise_table()
    before = prefix_2(step_gaps, ("steps", "inner"), add_terms, jnp.zeros((1,), jnp.int32))
    level_now = (window_start[0] - before[0]).astype(jnp.int32)
    level_next = level_now - step_gaps[0]
    window_count = lax.axis_size(("steps", "inner"))
    states = start_state
    drift = jnp.zeros_like(start_state)
    for iteration in range(ITERS):
        drift = drift_of(
            states,
            noise_draws[0],
            level_now,
            level_next,
            table,
            input_weight,
            embed_weight,
            first_weight,
            second_weight,
            output_weight,
        )
        blocks = drift.reshape(window_count, drift.size // window_count)
        columns = lax.all_to_all(
            blocks, ("steps", "inner"), split_axis=0, concat_axis=0, tiled=True
        )
        earlier_sums = jnp.cumsum(columns, axis=0) - columns
        returned = lax.all_to_all(
            earlier_sums, ("steps", "inner"), split_axis=0, concat_axis=0, tiled=True
        )
        prefix = returned.reshape(drift.shape)
        states = start_state + prefix
    return (states + drift)[None]


def solution(mesh):
    return jax.shard_map(
        shards,
        mesh=mesh,
        in_specs=(
            P("groups", None, None),
            P(("groups", "steps", "inner"), None, None, None),
            P(("groups", "steps", "inner")),
            P("groups"),
            P(),
            P(),
            P(),
            P(),
            P(),
        ),
        out_specs=P(("groups", "steps", "inner"), None, None, None),
        check_vma=False,
    )
```

profile of v0, /device:TPU:0, one launch (start us, length us, event | category | flops | bytes accessed | tf_op | source)
XLA Modules:
  0.0 191.9 jit_solution(16638882197625928342)
XLA Ops:
  3.4 13.8 %all-reduce.1 = s32[16]{0:T(128)S(1)} all-reduce(s32[16]{0:T(128)S(1)} %dynamic-update-slice), channel_id=2, replica_groups=mesh['groups'=2,'steps'=8,'inner'=2] {'steps','inner'}, use_global_device_ids=true, to_apply=%add.1 | all-reduce | flops 16 | bytes 128
  23.8 1.6 fusion.61
  28.6 1.7 fusion.59
  30.8 1.4 multiply_reduce_fusion.1
  32.6 1.5 subtract_multiply_fusion.1
  34.5 1.7 bitcast_reduce_fusion.2
  38.9 3.5 %fusion.52 = f32[8,32,768]{2,1,0:T(8,128)} fusion(f32[8,32,768]{2,1,0:T(8,128)} %param.11, bf16[8,32,1024]{2,1,0:T(8,128)(2,1)S(1)} %bitcast.187, bf16[1024,768]{1,0:T(8,128)(2,1)} %param.19, f32[1,8,32,768]{3,2,1,0:T(8,128)} %param.12, f32[]{:T(128)S(6)} %sqrt.28, f32[]{:T(128)S(6)} %mul.214, f32[]{:T(128)S(6)} %sqrt.12, f32[]{:T(128)S(6)} %sqrt.11, ...), kind=kOutput, calls=%fused_computation.71 | convolution fusion | flops 405209088 | bytes 4456468 | tf_op jit(solution)/shard_map/dot_general | solution.py:71
  42.4 1.9 %all_to_all.26 = f32[16,1,12288]{2,1,0:T(1,128)S(1)} reshape(f32[8,32,768]{2,1,0:T(8,128)} %fusion.52) | data formatting | bytes 1572864 | tf_op jit(solution)/shard_map/all_to_all | solution.py:139
  44.3 40.1 %all_to_all.32 = f32[16,1,12288]{2,1,0:T(1,128)S(1)} all-to-all(f32[16,1,12288]{2,1,0:T(1,128)S(1)} %all_to_all.26), channel_id=1, replica_groups=mesh['groups'=2,'steps'=8,'inner'=2] {'steps','inner'}, dimensions={0} | all-to-all | bytes 1572864 | tf_op jit(solution)/shard_map/all_to_all | solution.py:139
  85.0 24.1 %all_to_all.33 = f32[16,1,12288]{2,1,0:T(1,128)} all-to-all(f32[16,1,12288]{2,1,0:T(1,128)S(1)} %reduce-window_subtract_fusion.1), channel_id=1, replica_groups=mesh['groups'=2,'steps'=8,'inner'=2] {'steps','inner'}, dimensions={0} | all-to-all | bytes 1572864 | tf_op jit(solution)/shard_map/all_to_all | solution.py:143
  109.1 3.9 %reduce.1 = f32[16,12288]{1,0:T(8,128)} reduce(f32[16,1,12288]{2,1,0:T(1,128)} %all_to_all.33, f32[]{:T(128)} %constant.96), dimensions={1}, to_apply=%all_to_all.22.reduce_sub_computation | reduce | bytes 1572868 | tf_op jit(solution)/shard_map/all_to_all | solution.py:143
  112.9 2.1 %reshape.285 = f32[8,32,768]{2,1,0:T(8,128)} reshape(f32[16,12288]{1,0:T(8,128)} %reduce.1) | data formatting | bytes 1572864 | tf_op jit(solution)/shard_map/reshape | solution.py:146
  115.1 2.2 %fusion.58 = (bf16[8,32,768]{2,1,0:T(8,128)(2,1)S(1)}, f32[8,32,768]{2,1,0:T(8,128)}) fusion(f32[8,32,768]{2,1,0:T(8,128)S(1)} %copy-done.5, f32[8,32,768]{2,1,0:T(8,128)} %reshape.285), kind=kLoop, calls=%fused_computation.112 | loop fusion | flops 393216 | bytes 2752512 | tf_op jit(solution)/shard_map/convert_element_type | solution.py:55
  119.3 1.7 fusion.60
  121.5 1.4 multiply_reduce_fusion
  123.3 1.5 subtract_multiply_fusion
  125.2 1.7 bitcast_reduce_fusion
  129.6 3.5 %fusion.53 = f32[8,32,768]{2,1,0:T(8,128)} fusion(f32[8,32,768]{2,1,0:T(8,128)} %get-tuple-element.40, bf16[8,32,1024]{2,1,0:T(8,128)(2,1)S(1)} %bitcast.186, bf16[1024,768]{1,0:T(8,128)(2,1)} %param.19, f32[1,8,32,768]{3,2,1,0:T(8,128)} %param.12, f32[]{:T(128)S(6)} %sqrt.28, f32[]{:T(128)S(6)} %mul.214, f32[]{:T(128)S(6)} %sqrt.12, f32[]{:T(128)S(6)} %sqrt.11, ...), kind=kOutput, calls=%fused_computation.72 | convolution fusion | flops 405209088 | bytes 4456468 | tf_op jit(solution)/shard_map/dot_general | solution.py:71
  133.0 1.9 %all_to_all.27 = f32[16,1,12288]{2,1,0:T(1,128)S(1)} reshape(f32[8,32,768]{2,1,0:T(8,128)} %fusion.53) | data formatting | bytes 1572864 | tf_op jit(solution)/shard_map/all_to_all | solution.py:139
  135.0 23.9 %all_to_all.34 = f32[16,1,12288]{2,1,0:T(1,128)S(1)} all-to-all(f32[16,1,12288]{2,1,0:T(1,128)S(1)} %all_to_all.27), channel_id=1, replica_groups=mesh['groups'=2,'steps'=8,'inner'=2] {'steps','inner'}, dimensions={0} | all-to-all | bytes 1572864 | tf_op jit(solution)/shard_map/all_to_all | solution.py:139
  159.4 24.1 %all_to_all.35 = f32[16,1,12288]{2,1,0:T(1,128)} all-to-all(f32[16,1,12288]{2,1,0:T(1,128)S(1)} %reduce-window_subtract_fusion), channel_id=1, replica_groups=mesh['groups'=2,'steps'=8,'inner'=2] {'steps','inner'}, dimensions={0} | all-to-all | bytes 1572864 | tf_op jit(solution)/shard_map/all_to_all | solution.py:143
  183.5 3.9 %reduce.2 = f32[16,12288]{1,0:T(8,128)} reduce(f32[16,1,12288]{2,1,0:T(1,128)} %all_to_all.35, f32[]{:T(128)} %constant.96), dimensions={1}, to_apply=%all_to_all.25.reduce_sub_computation | reduce | bytes 1572868 | tf_op jit(solution)/shard_map/all_to_all | solution.py:143
  187.3 2.2 %reshape.289 = f32[8,32,768]{2,1,0:T(8,128)} reshape(f32[16,12288]{1,0:T(8,128)} %reduce.2) | data formatting | bytes 1572864 | tf_op jit(solution)/shard_map/reshape | solution.py:146
  189.5 2.4 %add_bitcast_fusion = f32[1,8,32,768]{3,2,1,0:T(8,128)} fusion(f32[8,32,768]{2,1,0:T(8,128)} %fusion.53, f32[8,32,768]{2,1,0:T(8,128)S(1)} %copy-done.6, f32[8,32,768]{2,1,0:T(8,128)} %reshape.289), kind=kLoop, calls=%fused_computation.73 | loop fusion | flops 393216 | bytes 3145728 | tf_op jit(solution)/shard_map/broadcast_in_dim | solution.py:148
  (121 shorter events, 16.9 us)
Async XLA Ops:
  0.0 28.6 %copy-start = (bf16[1024,1024]{1,0:T(8,128)(2,1)S(1)}, bf16[1024,1024]{1,0:T(8,128)(2,1)}, u32[]{:S(2)}) copy-start(bf16[1024,1024]{1,0:T(8,128)(2,1)} %param.17) | copy-start | bytes 6291460
  23.8 2.8 %copy-start.7 = (bf16[768,1024]{1,0:T(8,128)(2,1)S(1)}, bf16[768,1024]{1,0:T(8,128)(2,1)}, u32[]{:S(2)}) copy-start(bf16[768,1024]{1,0:T(8,128)(2,1)} %param.15) | copy-start | bytes 4718596
  32.6 1.9 copy-start.3
  36.3 2.3 %copy-start.2 = (f32[256,1024]{1,0:T(8,128)S(1)}, f32[256,1024]{1,0:T(8,128)}, u32[]{:S(2)}) copy-start(f32[256,1024]{1,0:T(8,128)} %get-tuple-element.48) | copy-start | bytes 3145732
  85.0 30.1 %copy-start.5 = (f32[8,32,768]{2,1,0:T(8,128)S(1)}, f32[8,32,768]{2,1,0:T(8,128)}, u32[]{:S(2)}) copy-start(f32[8,32,768]{2,1,0:T(8,128)} %param.11) | copy-start | bytes 2359300
  115.1 2.2 %copy-start.8 = (bf16[768,1024]{1,0:T(8,128)(2,1)S(1)}, bf16[768,1024]{1,0:T(8,128)(2,1)}, u32[]{:S(2)}) copy-start(bf16[768,1024]{1,0:T(8,128)(2,1)} %param.15) | copy-start | bytes 4718596
  123.3 1.9 copy-start.4
  126.9 2.3 %copy-start.1 = (f32[256,1024]{1,0:T(8,128)S(1)}, f32[256,1024]{1,0:T(8,128)}, u32[]{:S(2)}) copy-start(f32[256,1024]{1,0:T(8,128)} %get-tuple-element.54) | copy-start | bytes 3145732
  159.4 30.1 %copy-start.6 = (f32[8,32,768]{2,1,0:T(8,128)S(1)}, f32[8,32,768]{2,1,0:T(8,128)}, u32[]{:S(2)}) copy-start(f32[8,32,768]{2,1,0:T(8,128)} %param.11) | copy-start | bytes 2359300
where the time goes:
time: 193 us; the launch traced here: 192 us
  blocking collectives  126 us (65%)
  other arithmetic  28 us (15%)
  matrix products  16.6 us (9%)
  local copies, waits for them, and re-layouts  14 us (7%)
  between operations  7.37 us (4%)
    all_to_all x2, blocking collectives, shards(): lax.all_to_all(blocks, ('steps', 'inner'), split_axis=0, concat_axis=0, t...  64 us
    all_to_all x2, blocking collectives, shards(): lax.all_to_all(earlier_sums, ('steps', 'inner'), split_axis=0, concat_axi...  48.2 us
    unnamed x1, blocking collectives  13.8 us
    all_to_all x2, other arithmetic, shards(): lax.all_to_all(earlier_sums, ('steps', 'inner'), split_axis=0, concat_axi...  7.77 us
    dot_general x2, matrix products, predict_noise(): jnp.dot(act_three, output_weight, preferred_element_type=jnp.float32)  6.95 us
    reduce_sum x6, other arithmetic, group_mean(): jnp.mean(values, axis=1)  5.97 us
    reshape x2, local copies, waits for them, and re-layouts, shards(): prefix = returned.reshape(drift.shape)  4.29 us

commit v1 on v0

v1 whole, which is shorter than its diff:
```python
import math

import jax
import jax.numpy as jnp
from jax import lax
from jax.sharding import PartitionSpec as P

GROUPS = 32
ITERS = 2
TRAIN_STEPS = 1000
TIME = ("steps", "inner")


def noise_table():
    levels = jnp.arange(TRAIN_STEPS, dtype=jnp.float32)
    beta_values = 0.0001 + (0.02 - 0.0001) * levels / (TRAIN_STEPS - 1)
    return jnp.exp(jnp.cumsum(jnp.log1p(-beta_values)))


def lookup(table, levels):
    places = jnp.arange(TRAIN_STEPS, dtype=jnp.int32)
    return jnp.sum(jnp.where(places == levels[:, None], table, jnp.zeros_like(table)), axis=1)


def group_norm(hidden):
    times, patches, channels = hidden.shape

    def group_mean(values):
        per_channel = jnp.mean(values, axis=1).reshape(times, GROUPS, channels // GROUPS)
        per_group = jnp.mean(per_channel, axis=2, keepdims=True)
        return jnp.broadcast_to(per_group, per_channel.shape).reshape(times, 1, channels)

    offset = hidden - group_mean(hidden)
    return offset * lax.rsqrt(group_mean(offset * offset) + 1e-05)


def project(values, weight):
    return lax.dot_general(
        values.astype(jnp.bfloat16),
        weight,
        (((2,), (0,)), ((), ())),
        preferred_element_type=jnp.float32,
    )


def predict_noise(states, modulation, input_weight, first_weight, second_weight, output_weight):
    channels = input_weight.shape[1]
    scale_part = modulation[:, None, :channels]
    shift_part = modulation[:, None, channels:]
    entry = project(states, input_weight)
    act_one = jax.nn.silu(group_norm(entry) * (1.0 + scale_part) + shift_part)
    act_two = jax.nn.silu(group_norm(project(act_one, first_weight)))
    block = entry + project(act_two, second_weight)
    return project(jax.nn.silu(group_norm(block)), output_weight)


def shift_blocks(part, count, width, blocks):
    pairs = [(place, place + blocks * width) for place in range(count - blocks * width)]
    return lax.ppermute(part, TIME, pairs)


def earlier_blocks(part, count, width):
    total = shift_blocks(part, count, width, 1)
    reach = 1
    while reach < count // width - 1:
        total = total + shift_blocks(total, count, width, reach)
        reach *= 2
    return total


def shards(
    start_state,
    noise_draws,
    step_gaps,
    window_start,
    input_weight,
    embed_weight,
    first_weight,
    second_weight,
    output_weight,
):
    count = lax.axis_size(TIME)
    width = start_state.shape[0]
    assert count % width == 0
    groups = [list(range(first, first + width)) for first in range(0, count, width)]
    place = lax.axis_index(TIME)
    image = place % width
    first_time = place - image

    def exchange(values):
        return lax.all_to_all(values, TIME, 0, 0, axis_index_groups=groups, tiled=True)

    noise = exchange(noise_draws[0])
    later = jnp.arange(count + 1, dtype=jnp.int32) > place
    before = lax.psum(jnp.where(later, step_gaps[0], 0), TIME)
    marks = window_start[0] - lax.dynamic_slice_in_dim(before, first_time, width + 1)
    bars = lookup(noise_table(), marks)
    bar_now = bars[:-1, None, None]
    bar_next = bars[1:, None, None]
    half = embed_weight.shape[0] // 2
    frequency = jnp.exp(-math.log(10000.0) * jnp.arange(half, dtype=jnp.float32) / half)
    angles = marks[:-1, None].astype(jnp.float32) * frequency
    features = jnp.concatenate([jnp.cos(angles), jnp.sin(angles)], axis=1).astype(jnp.bfloat16)
    modulation = jnp.dot(features, embed_weight, preferred_element_type=jnp.float32)
    sigma = jnp.sqrt((1.0 - bar_next) / (1.0 - bar_now) * (1.0 - bar_now / bar_next))
    noise_coef = (1.0 - bar_next) * jnp.sqrt(bar_now / (bar_next * (1.0 - bar_now)))

    own = lax.dynamic_index_in_dim(start_state, image, 0, True)
    states = own
    for iteration in range(ITERS):
        predicted = predict_noise(
            states, modulation, input_weight, first_weight, second_weight, output_weight
        )
        clean = jnp.clip(
            (states - jnp.sqrt(1.0 - bar_now) * predicted) / jnp.sqrt(bar_now), -1.0, 1.0
        )
        implied = (states - jnp.sqrt(bar_now) * clean) / jnp.sqrt(1.0 - bar_now)
        drift = jnp.sqrt(bar_next) * clean + noise_coef * implied + sigma * noise - states
        totals = jnp.cumsum(drift, axis=0)
        base = own + earlier_blocks(totals[-1:], count, width)
        states = base + (totals - drift)
    return exchange(states + drift)[None]


def solution(mesh):
    return jax.shard_map(
        shards,
        mesh=mesh,
        in_specs=(
            P("groups", None, None),
            P(("groups", "steps", "inner"), None, None, None),
            P(("groups", "steps", "inner")),
            P("groups"),
            P(),
            P(),
            P(),
            P(),
            P(),
        ),
        out_specs=P(("groups", "steps", "inner"), None, None, None),
        check_vma=False,
    )
```

time: 193 us -> 87.7 us (0.45)
  blocking collectives: 126 us -> 33.3 us
  other arithmetic: 28 us -> 11 us
  starting transfers between devices: 0 us -> 12.6 us
  local copies, waits for them, and re-layouts: 14 us -> 5.39 us
  between operations: 7.37 us -> 1.9 us
  waiting for transfers between devices: 0 us -> 4.38 us
    all_to_all x4 -> x1, blocking collectives: 112 us -> 15.3 us  [exchange(): lax.all_to_all(values, TIME, 0, 0, axis_index_groups=groups, tiled=True)]
    psum x0 -> x1, blocking collectives: none -> 18 us  [shards(): before = lax.psum(jnp.where(later, step_gaps[0], 0), TIME)]
    unnamed x1 -> x0, blocking collectives: 13.8 us -> none
    all_to_all x2 -> x0, other arithmetic: 7.77 us -> none  [shards(): lax.all_to_all(earlier_sums, ('steps', 'inner'), split_axis=0, concat_axi...]
    ppermute x0 -> x2, starting transfers between devices: none -> 7.21 us  [shift_blocks(): return lax.ppermute(part, TIME, pairs)]
    all_to_all x0 -> x1, starting transfers between devices: none -> 5.42 us  [exchange(): lax.all_to_all(values, TIME, 0, 0, axis_index_groups=groups, tiled=True)]
    convert_element_type x8 -> x1, other arithmetic: 5.27 us -> 0.01 us  [shards(): angles = marks[:-1, None].astype(jnp.float32) * frequency]
    ppermute x0 -> x2, waiting for transfers between devices: none -> 4.38 us  [shift_blocks(): return lax.ppermute(part, TIME, pairs)]
  transfers between devices with their start and end apart: 0 -> 3, of which waited for: 0 -> 2; matrix products, arithmetic and copies ran while one was open for 0% -> 13% of each run, Pallas kernels for 0% -> 0%
where the time goes in v1:
time: 87.7 us; the launch traced here: 87.1 us
  blocking collectives  33.3 us (38%)
  matrix products  18.5 us (21%)
  starting transfers between devices  12.6 us (14%)
  other arithmetic  11 us (13%)
  local copies, waits for them, and re-layouts  5.39 us (6%)
  waiting for transfers between devices  4.38 us (5%)
  between operations  1.9 us (2%)
    psum x1, blocking collectives, shards(): before = lax.psum(jnp.where(later, step_gaps[0], 0), TIME)  18 us
    dot_general x8, matrix products, project(): lax.dot_general(values.astype(jnp.bfloat16), weight, (((2,), (0,)), ((),...  17.1 us
    all_to_all x1, blocking collectives, exchange(): lax.all_to_all(values, TIME, 0, 0, axis_index_groups=groups, tiled=True)  15.3 us
    ppermute x2, starting transfers between devices, shift_blocks(): return lax.ppermute(part, TIME, pairs)  7.21 us
    all_to_all x1, starting transfers between devices, exchange(): lax.all_to_all(values, TIME, 0, 0, axis_index_groups=groups, tiled=True)  5.42 us
    ppermute x2, waiting for transfers between devices, shift_blocks(): return lax.ppermute(part, TIME, pairs)  4.38 us
    another operation x2, other arithmetic, shards(): totals = jnp.cumsum(drift, axis=0)  3.39 us
    reduce_sum x6, other arithmetic, group_mean(): jnp.mean(values, axis=1).reshape(times, GROUPS, channels // GROUPS)  3.38 us
  transfers between devices with their start and end apart: 3, of which 2 were waited for; matrix products, arithmetic and copies ran while one was open for 13% of the time, Pallas kernels for 0%

profile of v1, /device:TPU:0, one launch (start us, length us, event | category | flops | bytes accessed | tf_op | source)
XLA Modules:
  0.0 87.1 jit_solution(368406443984099906)
XLA Ops:
  0.0 5.4 %all-to-all-start = ((f32[8,32,768]{2,1,0:T(8,128)}), f32[8,32,768]{2,1,0:T(8,128)}, u32[]{:S(2)}, u32[]{:S(2)}) async-start(f32[8,32,768]{2,1,0:T(8,128)} %bitcast.78), calls=%async_computation | async-start | bytes 1572864 | tf_op jit(solution)/shard_map/all_to_all | solution.py:91
  6.8 18.0 %psum.7 = s32[17]{0:T(128)S(1)} all-reduce(s32[17]{0:T(128)S(1)} %compare_select_fusion), channel_id=1, replica_groups=mesh['groups'=2,'steps'=8,'inner'=2] {'steps','inner'}, use_global_device_ids=true, to_apply=%region_0.1 | all-reduce | flops 17 | bytes 136 | tf_op jit(solution)/shard_map/psum | solution.py:95
  25.4 1.5 %fusion.75 = f32[8,2048]{1,0:T(8,128)S(1)} fusion(bf16[256,2048]{1,0:T(8,128)(2,1)} %param.14, bf16[8,128]{1,0:T(8,128)(2,1)S(1)} %get-tuple-element.8, bf16[8,128]{1,0:T(8,128)(2,1)S(1)} %get-tuple-element.7), kind=kOutput, calls=%fused_computation.87 | convolution fusion | flops 8396800 | bytes 1118208 | tf_op jit(solution)/shard_map/dot_general | solution.py:104
  26.8 1.9 %fusion.88 = (f32[1024]{0:T(1024)S(1)}, f32[32,1024]{1,0:T(8,128)S(1)}) fusion(bf16[768,1024]{1,0:T(8,128)(2,1)} %param.13, f32[8,32,768]{2,1,0:T(8,128)} %param.9, s32[]{:T(128)S(6)} %select_n.23), kind=kOutput, calls=%fused_computation.128 | convolution fusion | flops 50363392 | bytes 1757188 | tf_op jit(solution)/shard_map/dot_general | solution.py:38
  29.5 0.8 fusion.89
  31.4 2.7 %fusion.90 = (f32[8,1024]{1,0:T(8,128)S(1)}, f32[8,32,1024]{2,1,0:T(8,128)S(1)}) fusion(bf16[1024,1024]{1,0:T(8,128)(2,1)} %param.16, f32[8,32,1024]{2,1,0:T(8,128)} %copy-done.5, f32[8,1024]{1,0:T(8,128)S(1)} %rsqrt.75, f32[8,1024]{1,0:T(8,128)S(1)} %sub.131, f32[32,1024]{1,0:T(8,128)S(1)} %get-tuple-element.15), kind=kOutput, calls=%fused_computation.130 | convolution fusion | flops 539222016 | bytes 4423680 | tf_op jit(solution)/shard_map/dot_general | solution.py:38
  35.6 0.9 %dynamic-slice_bitcast_fusion = f32[32,768]{1,0:T(8,128)S(1)} fusion(f32[8,32,768]{2,1,0:T(8,128)} %param.9, s32[]{:T(128)S(6)} %select_n.23), kind=kLoop, calls=%fused_computation.66 | loop fusion | bytes 196612 | tf_op jit(solution)/shard_map/sub | solution.py:115
  36.6 2.5 %add_subtract_fusion.1 = f32[8,32,768]{2,1,0:T(8,128)S(1)} fusion(bf16[1024,768]{1,0:T(8,128)(2,1)} %param.17, f32[8,32,768]{2,1,0:T(8,128)} %all-to-all-done, f32[8,32,1024]{2,1,0:T(8,128)S(1)} %get-tuple-element.19, f32[8,1024]{1,0:T(8,128)S(1)} %rsqrt.77, f32[8,1024]{1,0:T(8,128)S(1)} %sub.134, f32[8]{0:T(128)S(1)} %get-tuple-element.11, ...), kind=kOutput, calls=%fused_computation.38 | convolution fusion | flops 407044096 | bytes 4358304 | tf_op jit(solution)/shard_map/dot_general | solution.py:38
  39.1 1.7 %fusion.94 = f32[8,32,768]{2,1,0:T(8,128)S(1)} fusion(f32[8,32,768]{2,1,0:T(8,128)S(1)} %add_subtract_fusion.1), kind=kOutput, calls=%fused_computation.134 | output fusion | flops 1376256 | bytes 1572864 | tf_op jit(solution)/shard_map/jit(cumsum)/reduce_window_sum | solution.py:119
  40.8 1.9 %collective-permute-start = (f32[1,32,768]{2,1,0:T(8,128)S(1)}, f32[1,32,768]{2,1,0:T(8,128)S(1)}, u32[]{:S(2)}, u32[]{:S(2)}) collective-permute-start(f32[1,32,768]{2,1,0:T(8,128)S(1)} %slice.46), channel_id=1, source_target_pairs={{0,8},{1,9},{2,10},{3,11},{4,12},{5,13},{6,14},{7,15},{16,24},{17,... | collective-permute-start | bytes 294920 | tf_op jit(solution)/shard_map/ppermute | solution.py:59
  42.7 2.2 %collective-permute-done = f32[1,32,768]{2,1,0:T(8,128)S(1)} collective-permute-done((f32[1,32,768]{2,1,0:T(8,128)S(1)}, f32[1,32,768]{2,1,0:T(8,128)S(1)}, u32[]{:S(2)}, u32[]{:S(2)}) %collective-permute-start) | collective-permute-done | bytes 98336 | tf_op jit(solution)/shard_map/ppermute | solution.py:59
  44.9 0.9 %add_bitcast_fusion.1 = f32[32,768]{1,0:T(8,128)S(1)} fusion(f32[1,32,768]{2,1,0:T(8,128)S(1)} %collective-permute-done, f32[8,32,768]{2,1,0:T(8,128)} %param.9, s32[]{:T(128)S(6)} %select_n.23), kind=kLoop, calls=%fused_computation.64 | loop fusion | flops 24576 | bytes 294916 | tf_op jit(solution)/shard_map/add | solution.py:121
  45.8 0.6 fusion.91
  47.5 1.9 %fusion.92 = (f32[8,1024]{1,0:T(8,128)S(1)}, f32[8,32,1024]{2,1,0:T(8,128)}) fusion(bf16[1024,1024]{1,0:T(8,128)(2,1)S(1)} %copy-done, f32[8,32,1024]{2,1,0:T(8,128)S(1)} %get-tuple-element.21, f32[8,1024]{1,0:T(8,128)S(1)} %rsqrt.79, f32[8,1024]{1,0:T(8,128)S(1)} %sub.143, f32[8,1024]{1,0:T(8,128)S(1)} %get-tuple-element.6, ...), kind=kOutput, calls=%fused_computation.132 | convolution fusion | flops 539484160 | bytes 4358144 | tf_op jit(solution)/shard_map/dot_general | solution.py:38
  49.8 1.4 %multiply_reduce_fusion.1 = f32[8,1024]{1,0:T(8,128)S(1)} fusion(f32[8,32,1024]{2,1,0:T(8,128)} %get-tuple-element.23, f32[8,1024]{1,0:T(8,128)S(1)} %sub.146), kind=kLoop, calls=%fused_computation.27 | loop fusion | flops 778240 | bytes 1114112 | tf_op jit(solution)/shard_map/reduce_sum | solution.py:29
  51.7 3.7 %fusion.93 = (f32[8,1024]{1,0:T(8,128)S(1)}, f32[8,32,1024]{2,1,0:T(8,128)}) fusion(f32[8,32,1024]{2,1,0:T(8,128)S(1)} %get-tuple-element.21, bf16[1024,1024]{1,0:T(8,128)(2,1)} %param.16, f32[8,32,1024]{2,1,0:T(8,128)} %get-tuple-element.23, f32[8,1024]{1,0:T(8,128)S(1)} %rsqrt.81, f32[8,1024]{1,0:T(8,128)S(1)} %sub.146), kind=kOutput, calls=%fused_computation.133 | convolution fusion | flops 539222016 | bytes 5341184 | tf_op jit(solution)/shard_map/dot_general | solution.py:38
  55.8 1.4 %multiply_reduce_fusion = f32[8,1024]{1,0:T(8,128)S(1)} fusion(f32[8,32,1024]{2,1,0:T(8,128)} %get-tuple-element.25, f32[8,1024]{1,0:T(8,128)S(1)} %sub.149), kind=kLoop, calls=%fused_computation.25 | loop fusion | flops 778240 | bytes 1114112 | tf_op jit(solution)/shard_map/reduce_sum | solution.py:29
  57.7 3.1 %add_subtract_fusion = f32[8,32,768]{2,1,0:T(8,128)S(1)} fusion(bf16[1024,768]{1,0:T(8,128)(2,1)} %param.17, f32[8,32,768]{2,1,0:T(8,128)} %all-to-all-done, f32[8,32,1024]{2,1,0:T(8,128)} %get-tuple-element.25, f32[8,1024]{1,0:T(8,128)S(1)} %rsqrt.83, f32[8,1024]{1,0:T(8,128)S(1)} %sub.149, f32[8]{0:T(128)S(1)} %get-tuple-element.11, ...), kind=kOutput, calls=%fused_computation.36 | convolution fusion | flops 407437312 | bytes 5931168 | tf_op jit(solution)/shard_map/dot_general | solution.py:38
  60.7 1.7 %fusion.95 = f32[8,32,768]{2,1,0:T(8,128)S(1)} fusion(f32[8,32,768]{2,1,0:T(8,128)S(1)} %add_subtract_fusion), kind=kOutput, calls=%fused_computation.135 | output fusion | flops 1376256 | bytes 1572864 | tf_op jit(solution)/shard_map/jit(cumsum)/reduce_window_sum | solution.py:119
  62.4 5.3 %collective-permute-start.1 = (f32[1,32,768]{2,1,0:T(8,128)S(1)}, f32[1,32,768]{2,1,0:T(8,128)S(1)}, u32[]{:S(2)}, u32[]{:S(2)}) collective-permute-start(f32[1,32,768]{2,1,0:T(8,128)S(1)} %slice.47), channel_id=1, source_target_pairs={{0,8},{1,9},{2,10},{3,11},{4,12},{5,13},{6,14},{7,15},{16,24},{17,... | collective-permute-start | bytes 294920 | tf_op jit(solution)/shard_map/ppermute | solution.py:59
  67.8 2.2 %collective-permute-done.1 = f32[1,32,768]{2,1,0:T(8,128)S(1)} collective-permute-done((f32[1,32,768]{2,1,0:T(8,128)S(1)}, f32[1,32,768]{2,1,0:T(8,128)S(1)}, u32[]{:S(2)}, u32[]{:S(2)}) %collective-permute-start.1) | collective-permute-done | bytes 98336 | tf_op jit(solution)/shard_map/ppermute | solution.py:59
  69.9 0.9 %add_bitcast_fusion = f32[32,768]{1,0:T(8,128)S(1)} fusion(f32[1,32,768]{2,1,0:T(8,128)S(1)} %collective-permute-done.1, f32[8,32,768]{2,1,0:T(8,128)} %param.9, s32[]{:T(128)S(6)} %select_n.23), kind=kLoop, calls=%fused_computation.63 | loop fusion | flops 24576 | bytes 294916 | tf_op jit(solution)/shard_map/add | solution.py:121
  71.0 15.3 %all_to_all.10 = f32[8,32,768]{2,1,0:T(8,128)S(1)} all-to-all(f32[8,32,768]{2,1,0:T(8,128)S(1)} %add_add_fusion), channel_id=1, replica_groups={{0,1,2,3,4,5,6,7},{8,9,10,11,12,13,14,15},{16,17,18,19,20,21,22,23},{24..., dimensions={0} | all-to-all | bytes 1572864 | tf_op jit(solution)/shard_map/all_to_all | solution.py:91
  86.3 0.9 %copy.13 = f32[1,8,32,768]{3,2,1,0:T(8,128)} copy(f32[1,8,32,768]{3,2,1,0:T(8,128)S(1)} %bitcast.77) | data formatting | bytes 1572864
  (109 shorter events, 6.6 us)
Async XLA Ops:
  0.0 29.5 %copy-start = (bf16[1024,1024]{1,0:T(8,128)(2,1)S(1)}, bf16[1024,1024]{1,0:T(8,128)(2,1)}, u32[]{:S(2)}) copy-start(bf16[1024,1024]{1,0:T(8,128)(2,1)} %param.15) | copy-start | bytes 6291460
  0.0 36.6 %all-to-all-start = ((f32[8,32,768]{2,1,0:T(8,128)}), f32[8,32,768]{2,1,0:T(8,128)}, u32[]{:S(2)}, u32[]{:S(2)}) async-start(f32[8,32,768]{2,1,0:T(8,128)} %bitcast.78), calls=%async_computation | async-start | bytes 1572864 | tf_op jit(solution)/shard_map/all_to_all | solution.py:91
  30.3 1.0 %copy-start.5 = (f32[8,32,1024]{2,1,0:T(8,128)}, f32[8,32,1024]{2,1,0:T(8,128)S(1)}, u32[]{:S(2)}) copy-start(f32[8,32,1024]{2,1,0:T(8,128)S(1)} %get-tuple-element.17) | copy-start | bytes 3145732
  39.0 7.4 %copy-start.4 = (f32[8,32,768]{2,1,0:T(8,128)}, f32[8,32,768]{2,1,0:T(8,128)S(1)}, u32[]{:S(2)}) copy-start(f32[8,32,768]{2,1,0:T(8,128)S(1)} %add_subtract_fusion.1) | copy-start | bytes 2359300
  39.1 6.8 %copy-start.1 = (bf16[768,1024]{1,0:T(8,128)(2,1)S(1)}, bf16[768,1024]{1,0:T(8,128)(2,1)}, u32[]{:S(2)}) copy-start(bf16[768,1024]{1,0:T(8,128)(2,1)} %param.13) | copy-start | bytes 4718596
  40.8 5.7 %copy-start.2 = (f32[8,32,768]{2,1,0:T(8,128)}, f32[8,32,768]{2,1,0:T(8,128)S(1)}, u32[]{:S(2)}) copy-start(f32[8,32,768]{2,1,0:T(8,128)S(1)} %fusion.94) | copy-start | bytes 2359300
  40.8 4.1 %collective-permute-start = (f32[1,32,768]{2,1,0:T(8,128)S(1)}, f32[1,32,768]{2,1,0:T(8,128)S(1)}, u32[]{:S(2)}, u32[]{:S(2)}) collective-permute-start(f32[1,32,768]{2,1,0:T(8,128)S(1)} %slice.46), channel_id=1, source_target_pairs={{0,8},{1,9},{2,10},{3,11},{4,12},{5,13},{6,14},{7,15},{16,24},{17,... | collective-permute-start | bytes 294920 | tf_op jit(solution)/shard_map/ppermute | solution.py:59
  55.4 2.3 %copy-start.3 = (f32[8,32,768]{2,1,0:T(8,128)S(1)}, f32[8,32,768]{2,1,0:T(8,128)}, u32[]{:S(2)}) copy-start(f32[8,32,768]{2,1,0:T(8,128)} %copy-done.2) | copy-start | bytes 2359300
  62.4 7.5 %collective-permute-start.1 = (f32[1,32,768]{2,1,0:T(8,128)S(1)}, f32[1,32,768]{2,1,0:T(8,128)S(1)}, u32[]{:S(2)}, u32[]{:S(2)}) collective-permute-start(f32[1,32,768]{2,1,0:T(8,128)S(1)} %slice.47), channel_id=1, source_target_pairs={{0,8},{1,9},{2,10},{3,11},{4,12},{5,13},{6,14},{7,15},{16,24},{17,... | collective-permute-start | bytes 294920 | tf_op jit(solution)/shard_map/ppermute | solution.py:59

commit v2 on v1

v2 whole, which is shorter than its diff:
```python
import functools
import math

import jax
import jax.numpy as jnp
import numpy as np
from jax import lax
from jax.experimental import pallas as pl
from jax.experimental.pallas import tpu as pltpu
from jax.sharding import PartitionSpec as P

GROUPS = 32
TRAIN_STEPS = 1000
TIME = ("steps", "inner")
LANES = 128
CHUNK = 256
COEFS = 5


def noise_table():
    levels = np.arange(TRAIN_STEPS, dtype=np.float64)
    betas = 0.0001 + (0.02 - 0.0001) * levels / (TRAIN_STEPS - 1)
    padded = np.zeros((1, -(-TRAIN_STEPS // LANES) * LANES), np.float32)
    padded[0, :TRAIN_STEPS] = np.exp(np.cumsum(np.log1p(-betas)))
    return padded


def group_mean(sums, size, count):
    lane = lax.broadcasted_iota(jnp.int32, sums.shape, 1)
    reach = 1
    while reach < size:
        upper = (lane & reach) != 0
        sums = sums + jnp.where(
            upper, pltpu.roll(sums, reach, 1), pltpu.roll(sums, LANES - reach, 1)
        )
        reach *= 2
    return sums * (1.0 / count)


def norm_silu(hidden_ref, act_ref, first, times, size, scale_ref, shift_ref):
    rows = hidden_ref.shape[0]
    patches = rows // times
    for lane in range(first, first + CHUNK, LANES):
        columns = slice(lane, lane + LANES)
        values = hidden_ref[:, columns].reshape(patches, times, LANES)
        mean = group_mean(jnp.sum(values, axis=0), size, patches * size)
        offset = values - mean
        spread = group_mean(jnp.sum(offset * offset, axis=0), size, patches * size)
        gain = 0.5 * lax.rsqrt(spread + 1e-05)
        if scale_ref is None:
            half = offset * gain
        else:
            gain = gain * (1.0 + scale_ref[:, columns])
            half = offset * gain + 0.5 * shift_ref[:, columns]
        act = half * jnp.tanh(half) + half
        act_ref[:, columns] = act.reshape(rows, LANES).astype(jnp.bfloat16)


def dot(left, right):
    return jnp.dot(left, right, preferred_element_type=jnp.float32)


def network(times, rows_ref, scale_ref, shift_ref, weights, entry_ref, hidden_ref, one_ref, two_ref, eps_ref):
    input_weight, first_weight, second_weight, output_weight = weights
    features, channels = input_weight.shape
    size = channels // GROUPS
    flat = jnp.concatenate([rows_ref[block] for block in range(features // LANES)], axis=1)
    flat = flat.astype(jnp.bfloat16)
    for first in range(0, channels, CHUNK):
        columns = slice(first, first + CHUNK)
        entry_ref[:, columns] = dot(flat, input_weight[:, columns])
        norm_silu(entry_ref, one_ref, first, times, size, scale_ref, shift_ref)
    for first in range(0, channels, CHUNK):
        columns = slice(first, first + CHUNK)
        hidden_ref[:, columns] = dot(one_ref[...], first_weight[:, columns])
        norm_silu(hidden_ref, two_ref, first, times, size, None, None)
    for first in range(0, channels, CHUNK):
        columns = slice(first, first + CHUNK)
        hidden_ref[:, columns] = entry_ref[:, columns] + dot(
            two_ref[...], second_weight[:, columns]
        )
        norm_silu(hidden_ref, one_ref, first, times, size, None, None)
    for first in range(0, features, CHUNK):
        part = dot(one_ref[...], output_weight[:, first : first + CHUNK])
        for lane in range(0, CHUNK, LANES):
            eps_ref[(first + lane) // LANES] = part[:, lane : lane + LANES]


def coefficients(now, later):
    ratio = (1.0 - later) / (1.0 - now)
    keep = ratio * jnp.sqrt(now / later)
    return (
        1.0 / jnp.sqrt(now),
        jnp.sqrt((1.0 - now) / now),
        (later - now) / (jnp.sqrt(later) * (1.0 - now)),
        keep - 1.0,
        jnp.sqrt(ratio * (1.0 - now / later)),
    )


def drift(state, eps, noise, coefs):
    inverse, slope, clean_part, state_part, sigma = coefs
    clean = jnp.clip(inverse * state - slope * eps, -1.0, 1.0)
    return clean_part * clean + state_part * state + sigma * noise


def spread_rows(rows_ref, step, stride, values):
    patches, features = values.shape
    for block in range(features // LANES):
        part = values[:, block * LANES : (block + 1) * LANES]
        rows_ref[block, pl.ds(step, patches, stride), :] = part


def first_kernel(
    width,
    start_ref,
    noise_ref,
    marks_ref,
    table_ref,
    input_ref,
    embed_ref,
    first_ref,
    second_ref,
    output_ref,
    state_ref,
    total_ref,
    scale_ref,
    shift_ref,
    coef_ref,
    own_ref,
    noise_buf,
    rows_ref,
    entry_ref,
    hidden_ref,
    one_ref,
    two_ref,
    eps_ref,
    sems,
):
    place = lax.axis_index(TIME)
    image = lax.rem(place, width)
    own_copy = pltpu.make_async_copy(start_ref.at[image], own_ref, sems.at[0])
    own_copy.start()
    noise_copy = pltpu.make_async_copy(noise_ref, noise_buf, sems.at[1])
    noise_copy.start()

    patches, features = own_ref.shape
    lane = lax.broadcasted_iota(jnp.int32, (width, marks_ref.shape[1]), 1)
    time = lax.broadcasted_iota(jnp.int32, lane.shape, 0)
    marks = marks_ref[...].astype(jnp.float32)
    spot = place - image + time
    now_mark = jnp.sum(jnp.where(lane == spot, marks, 0.0), axis=1, keepdims=True)
    next_mark = jnp.sum(jnp.where(lane == spot + 1, marks, 0.0), axis=1, keepdims=True)
    level = lax.broadcasted_iota(jnp.int32, (width, table_ref.shape[1]), 1).astype(jnp.float32)
    table = table_ref[...]
    now = jnp.sum(jnp.where(level == now_mark, table, 0.0), axis=1, keepdims=True)
    later = jnp.sum(jnp.where(level == next_mark, table, 0.0), axis=1, keepdims=True)
    coefs = coefficients(now, later)
    for index, coef in enumerate(coefs):
        coef_ref[index] = jnp.broadcast_to(coef, (width, LANES))

    half = embed_ref.shape[0] // 2
    order = lax.broadcasted_iota(jnp.int32, (1, half), 1).astype(jnp.float32)
    angles = now_mark * jnp.exp(-math.log(10000.0) * order / half)
    channels = input_ref.shape[1]
    cosine = jnp.cos(angles).astype(jnp.bfloat16)
    sine = jnp.sin(angles).astype(jnp.bfloat16)
    both = jnp.concatenate([cosine, sine], axis=1)
    scale_ref[...] = dot(both, embed_ref[:, :channels])
    shift_ref[...] = dot(both, embed_ref[:, channels:])

    own_copy.wait()
    own = own_ref[...]
    for step in range(width):
        spread_rows(rows_ref, step, width, own)
    weights = (input_ref, first_ref, second_ref, output_ref)
    network(
        width, rows_ref, scale_ref, shift_ref, weights, entry_ref, hidden_ref, one_ref, two_ref, eps_ref
    )
    noise_copy.wait()
    for block in range(features // LANES):
        columns = slice(block * LANES, (block + 1) * LANES)
        base = own_ref[:, columns]
        running = None
        for step in range(width):
            eps = eps_ref[block, pl.ds(step, patches, width), :]
            row = [coef_ref[index, step : step + 1, :] for index in range(COEFS)]
            state_ref[step, :, columns] = base if running is None else base + running
            change = drift(base, eps, noise_buf[step, :, columns], row)
            running = change if running is None else running + change
        total_ref[:, columns] = running


def second_kernel(
    width,
    state_ref,
    earlier_ref,
    noise_ref,
    scale_ref,
    shift_ref,
    coef_ref,
    input_ref,
    first_ref,
    second_ref,
    output_ref,
    sum_ref,
    total_ref,
    noise_buf,
    rows_ref,
    entry_ref,
    hidden_ref,
    one_ref,
    two_ref,
    eps_ref,
    sems,
):
    noise_copy = pltpu.make_async_copy(noise_ref, noise_buf, sems.at[0])
    noise_copy.start()
    patches, features = earlier_ref.shape
    for step in range(width):
        spread_rows(rows_ref, step, width, state_ref[step] + earlier_ref[...])
    weights = (input_ref, first_ref, second_ref, output_ref)
    network(
        width, rows_ref, scale_ref, shift_ref, weights, entry_ref, hidden_ref, one_ref, two_ref, eps_ref
    )
    noise_copy.wait()
    for block in range(features // LANES):
        columns = slice(block * LANES, (block + 1) * LANES)
        own = state_ref[0, :, columns]
        running = None
        for step in range(width):
            eps = eps_ref[block, pl.ds(step, patches, width), :]
            row = [coef_ref[index, step : step + 1, :] for index in range(COEFS)]
            state = state_ref[step, :, columns] + earlier_ref[:, columns]
            change = drift(state, eps, noise_buf[step, :, columns], row)
            running = change if running is None else running + change
            sum_ref[step, :, columns] = own + running
        total_ref[:, columns] = running


def shift_blocks(part, count, width, blocks):
    pairs = [(place, place + blocks * width) for place in range(count - blocks * width)]
    return lax.ppermute(part, TIME, pairs)


def earlier_blocks(part, count, width):
    total = shift_blocks(part, count, width, 1)
    reach = 1
    while reach < count // width - 1:
        total = total + shift_blocks(total, count, width, reach)
        reach *= 2
    return total


def shards(
    start_state,
    noise_draws,
    step_gaps,
    window_start,
    input_weight,
    embed_weight,
    first_weight,
    second_weight,
    output_weight,
):
    count = lax.axis_size(TIME)
    width, patches, features = start_state.shape
    channels = input_weight.shape[1]
    assert count % width == 0 and width % 8 == 0
    groups = [list(range(first, first + width)) for first in range(0, count, width)]
    place = lax.axis_index(TIME)

    def exchange(values):
        return lax.all_to_all(values, TIME, 0, 0, axis_index_groups=groups, tiled=True)

    noise = exchange(noise_draws[0])
    marks_length = -(-(count + 1) // LANES) * LANES
    later = jnp.arange(marks_length, dtype=jnp.int32) > place
    opening = jnp.where(place == 0, window_start[0], 0)
    marks = lax.psum(opening - jnp.where(later, step_gaps[0], 0), TIME)[None]

    def shape(*dims):
        return jax.ShapeDtypeStruct(dims, jnp.float32)

    vmem = pl.BlockSpec(memory_space=pltpu.VMEM)
    anywhere = pl.BlockSpec(memory_space=pl.ANY)
    rows = width * patches
    work = [
        pltpu.VMEM((width, patches, features), jnp.float32),
        pltpu.VMEM((features // LANES, rows, LANES), jnp.float32),
        pltpu.VMEM((rows, channels), jnp.float32),
        pltpu.VMEM((rows, channels), jnp.float32),
        pltpu.VMEM((rows, channels), jnp.bfloat16),
        pltpu.VMEM((rows, channels), jnp.bfloat16),
        pltpu.VMEM((features // LANES, rows, LANES), jnp.float32),
        pltpu.SemaphoreType.DMA((2,)),
    ]
    params = pltpu.CompilerParams(vmem_limit_bytes=24 * 2**20)
    states, total, scale, shift, coefs = pl.pallas_call(
        functools.partial(first_kernel, width),
        out_shape=(
            shape(width, patches, features),
            shape(patches, features),
            shape(width, channels),
            shape(width, channels),
            shape(COEFS, width, LANES),
        ),
        in_specs=[anywhere, anywhere] + [vmem] * 7,
        out_specs=(vmem,) * 5,
        scratch_shapes=[pltpu.VMEM((patches, features), jnp.float32)] + work,
        compiler_params=params,
        name="first",
    )(
        start_state,
        noise,
        marks,
        jnp.asarray(noise_table()),
        input_weight,
        embed_weight,
        first_weight,
        second_weight,
        output_weight,
    )
    sums, total = pl.pallas_call(
        functools.partial(second_kernel, width),
        out_shape=(shape(width, patches, features), shape(patches, features)),
        in_specs=[vmem, vmem, anywhere] + [vmem] * 7,
        out_specs=(vmem,) * 2,
        scratch_shapes=work,
        compiler_params=params,
        name="second",
    )(
        states,
        earlier_blocks(total, count, width),
        noise,
        scale,
        shift,
        coefs,
        input_weight,
        first_weight,
        second_weight,
        output_weight,
    )
    return exchange(sums + earlier_blocks(total, count, width))[None]


def solution(mesh):
    return jax.shard_map(
        shards,
        mesh=mesh,
        in_specs=(
            P("groups", None, None),
            P(("groups", "steps", "inner"), None, None, None),
            P(("groups", "steps", "inner")),
            P("groups"),
            P(),
            P(),
            P(),
            P(),
            P(),
        ),
        out_specs=P(("groups", "steps", "inner"), None, None, None),
        check_vma=False,
    )
```

time: 87.7 us -> 72.1 us (0.82)
  matrix products: 18.5 us -> 0 us
  Pallas kernels: 0 us -> 11.4 us
  other arithmetic: 11 us -> 0.07 us
  local copies, waits for them, and re-layouts: 5.39 us -> 8.52 us
    dot_general x9 -> x0, matrix products: 18.5 us -> none  [the longest x8 17.1 us: project(): lax.dot_general(values.astype(jnp.bfloat16), weight, (((2,), (0,)), ((),...]
    pallas_call x0 -> x2, Pallas kernels: none -> 11.4 us  [the longest x1 5.91 us: shards(): pl.pallas_call(functools.partial(first_kernel, width), out_shape=(shape(w...]
    unnamed x13 -> x19, local copies, waits for them, and re-layouts: 0.93 us -> 8.52 us
    reduce_sum x19 -> x0, other arithmetic: 4.86 us -> none  [the longest x6 3.38 us: group_mean(): jnp.mean(values, axis=1).reshape(times, GROUPS, channels // GROUPS)]
    another operation x6 -> x0, other arithmetic: 3.88 us -> none  [the longest x2 3.39 us: shards(): totals = jnp.cumsum(drift, axis=0)]
    add x4 -> x1, other arithmetic: 1.93 us -> 0.06 us  [shards(): return exchange(sums + earlier_blocks(total, count, width))[None]]
    sub x6 -> x0, local copies, waits for them, and re-layouts: 1.44 us -> none  [the longest x1 0.91 us: shards(): states - jnp.sqrt(1.0 - bar_now) * predicted]
    broadcast_in_dim x13 -> x0, local copies, waits for them, and re-layouts: 1.13 us -> none  [group_mean(): jnp.broadcast_to(per_group, per_channel.shape).reshape(times, 1, channels)]
  transfers between devices with their start and end apart: 3 -> 3, of which waited for: 2 -> 2; matrix products, arithmetic and copies ran while one was open for 13% -> 0% of each run, Pallas kernels for 0% -> 0%
where the time goes in v2:
time: 72.1 us; the launch traced here: 71.6 us
  blocking collectives  33 us (46%)
  starting transfers between devices  12.9 us (18%)
  Pallas kernels  11.4 us (16%)
  local copies, waits for them, and re-layouts  8.52 us (12%)
  waiting for transfers between devices  4.38 us (6%)
  between operations  1.37 us (2%)
    psum x1, blocking collectives, shards(): marks = lax.psum(opening - jnp.where(later, step_gaps[0], 0), TIME)[None]  17.7 us
    all_to_all x1, blocking collectives, exchange(): lax.all_to_all(values, TIME, 0, 0, axis_index_groups=groups, tiled=True)  15.3 us
    unnamed x19, local copies, waits for them, and re-layouts  8.52 us
    ppermute x2, starting transfers between devices, shift_blocks(): return lax.ppermute(part, TIME, pairs)  7.51 us
    pallas_call x1, Pallas kernels, shards(): pl.pallas_call(functools.partial(first_kernel, width), out_shape=(shape(w...  5.91 us
    pallas_call x1, Pallas kernels, shards(): pl.pallas_call(functools.partial(second_kernel, width), out_shape=(shape(...  5.46 us
    all_to_all x1, starting transfers between devices, exchange(): lax.all_to_all(values, TIME, 0, 0, axis_index_groups=groups, tiled=True)  5.42 us
    ppermute x2, waiting for transfers between devices, shift_blocks(): return lax.ppermute(part, TIME, pairs)  4.38 us
  transfers between devices with their start and end apart: 3, of which 2 were waited for; matrix products, arithmetic and copies ran while one was open for 0% of the time, Pallas kernels for 0%

profile of v2, /device:TPU:0, one launch (start us, length us, event | category | flops | bytes accessed | tf_op | source)
XLA Modules:
  0.0 71.6 jit_solution(17385071535617548734)
XLA Ops:
  0.0 0.0 copy-start.4
  0.0 5.4 %all-to-all-start = ((f32[8,32,768]{2,1,0:T(8,128)}), f32[8,32,768]{2,1,0:T(8,128)S(1)}, u32[]{:S(2)}, u32[]{:S(2)}) async-start(f32[8,32,768]{2,1,0:T(8,128)} %bitcast.9), calls=%async_computation | async-start | bytes 1572864 | tf_op jit(solution)/shard_map/all_to_all | solution.py:274
  6.7 17.7 %psum.7.marks_ref = s32[1,128]{1,0:T(1,128)S(1)} all-reduce(s32[1,128]{1,0:T(1,128)S(1)} %fusion.1), channel_id=1, replica_groups=mesh['groups'=2,'steps'=8,'inner'=2] {'steps','inner'}, use_global_device_ids=true, to_apply=%region_0.1 | all-reduce | flops 128 | bytes 1024 | tf_op jit(solution)/shard_map/psum | solution.py:280
  24.4 0.0 all-to-all-done.noise_ref
  24.4 0.0 copy-done.4
  24.4 0.0 copy-start
  24.4 1.6 %copy-done = bf16[1024,1024]{1,0:T(8,128)(2,1)S(1)} copy-done((bf16[1024,1024]{1,0:T(8,128)(2,1)S(1)}, bf16[1024,1024]{1,0:T(8,128)(2,1)}, u32[]{:S(2)}) %copy-start) | copy-done | bytes 2097176
  26.0 0.0 copy-start.2
  26.0 1.6 %copy-done.2 = bf16[1024,1024]{1,0:T(8,128)(2,1)S(1)} copy-done((bf16[1024,1024]{1,0:T(8,128)(2,1)S(1)}, bf16[1024,1024]{1,0:T(8,128)(2,1)}, u32[]{:S(2)}) %copy-start.2) | copy-done | bytes 2097176
  27.6 1.4 %copy-done.5 = bf16[1024,768]{1,0:T(8,128)(2,1)S(1)} copy-done((bf16[1024,768]{1,0:T(8,128)(2,1)S(1)}, bf16[1024,768]{1,0:T(8,128)(2,1)}, u32[]{:S(2)}) %copy-start.5) | copy-done | bytes 1572888
  29.0 1.2 %copy-done.6 = bf16[256,2048]{1,0:T(8,128)(2,1)S(1)} copy-done((bf16[256,2048]{1,0:T(8,128)(2,1)S(1)}, bf16[256,2048]{1,0:T(8,128)(2,1)}, u32[]{:S(2)}) %copy-start.6) | copy-done | bytes 1048600
  30.2 1.1 %copy-done.7 = f32[8,32,768]{2,1,0:T(8,128)S(1)} copy-done((f32[8,32,768]{2,1,0:T(8,128)S(1)}, f32[8,32,768]{2,1,0:T(8,128)}, u32[]{:S(2)}) %copy-start.7) | copy-done | bytes 786456
  31.4 0.7 copy-done.8
  32.1 5.9 %first.1 = (f32[8,32,768]{2,1,0:T(8,128)S(1)}, f32[32,768]{1,0:T(8,128)S(1)}, f32[8,1024]{1,0:T(8,128)S(1)}, f32[8,1024]{1,0:T(8,128)S(1)}, f32[5,8,128]{2,1,0:T(8,128)S(1)}) custom-call(f32[8,32,768]{2,1,0:T(8,128)S(1)} %copy-done.7, f32[8,32,768]{2,1,0:T(8,128)S(1)} %all-to-all-done.noise_ref, s32[1,128]{1,0:T(1,128)S(1)} %psum.7.marks_ref, ...), custom_call_target="tpu_custom_call" | custom-call | tf_op jit(solution)/shard_map/first/pallas_call | solution.py:299
  38.0 2.2 %collective-permute-start = (f32[32,768]{1,0:T(8,128)S(1)}, f32[32,768]{1,0:T(8,128)S(1)}, u32[]{:S(2)}, u32[]{:S(2)}) collective-permute-start(f32[32,768]{1,0:T(8,128)S(1)} %get-tuple-element.13), channel_id=1, source_target_pairs={{0,8},{1,9},{2,10},{3,11},{4,12},{5,13},{6,14},{7,15},{16,24},{17,... | collective-permute-start | bytes 294920 | tf_op jit(solution)/shard_map/ppermute | solution.py:243
  40.2 2.2 %collective-permute-done.earlier_ref = f32[32,768]{1,0:T(8,128)S(1)} collective-permute-done((f32[32,768]{1,0:T(8,128)S(1)}, f32[32,768]{1,0:T(8,128)S(1)}, u32[]{:S(2)}, u32[]{:S(2)}) %collective-permute-start) | collective-permute-done | bytes 98336 | tf_op jit(solution)/shard_map/ppermute | solution.py:243
  42.4 0.0 copy-done.1
  42.4 0.0 copy-done.3
  42.4 5.5 %second.1 = (f32[8,32,768]{2,1,0:T(8,128)S(1)}, f32[32,768]{1,0:T(8,128)S(1)}) custom-call(f32[8,32,768]{2,1,0:T(8,128)S(1)} %get-tuple-element.12.state_ref, f32[32,768]{1,0:T(8,128)S(1)} %collective-permute-done.earlier_ref, f32[8,32,768]{2,1,0:T(8,128)S(1)} %all-to-all-done.noise_ref, f32[8,1024]{1,0:T(8,128)S(1)} %get-tuple-element.14.scale_ref, ...), custom_call_target="tpu_custom_call" | custom-call | tf_op jit(solution)/shard_map/second/pallas_call | solution.py:324
  47.9 5.3 %collective-permute-start.1 = (f32[32,768]{1,0:T(8,128)S(1)}, f32[32,768]{1,0:T(8,128)S(1)}, u32[]{:S(2)}, u32[]{:S(2)}) collective-permute-start(f32[32,768]{1,0:T(8,128)S(1)} %get-tuple-element.18), channel_id=1, source_target_pairs={{0,8},{1,9},{2,10},{3,11},{4,12},{5,13},{6,14},{7,15},{16,24},{17,... | collective-permute-start | bytes 294920 | tf_op jit(solution)/shard_map/ppermute | solution.py:243
  53.2 2.2 %collective-permute-done.1 = f32[32,768]{1,0:T(8,128)S(1)} collective-permute-done((f32[32,768]{1,0:T(8,128)S(1)}, f32[32,768]{1,0:T(8,128)S(1)}, u32[]{:S(2)}, u32[]{:S(2)}) %collective-permute-start.1) | collective-permute-done | bytes 98336 | tf_op jit(solution)/shard_map/ppermute | solution.py:243
  55.3 0.1 broadcast_add_fusion
  55.4 15.3 %all_to_all.10 = f32[8,32,768]{2,1,0:T(8,128)S(1)} all-to-all(f32[8,32,768]{2,1,0:T(8,128)S(1)} %broadcast_add_fusion), channel_id=1, replica_groups={{0,1,2,3,4,5,6,7},{8,9,10,11,12,13,14,15},{16,17,18,19,20,21,22,23},{24..., dimensions={0} | all-to-all | bytes 1572864 | tf_op jit(solution)/shard_map/all_to_all | solution.py:274
  70.7 0.9 %copy.14 = f32[1,8,32,768]{3,2,1,0:T(8,128)} copy(f32[1,8,32,768]{3,2,1,0:T(8,128)S(1)} %bitcast.8) | data formatting | bytes 1572864
  (7 shorter events, 0.0 us)
Async XLA Ops:
  0.0 24.4 %copy-start.4 = (bf16[768,1024]{1,0:T(8,128)(2,1)S(1)}, bf16[768,1024]{1,0:T(8,128)(2,1)}, u32[]{:S(2)}) copy-start(bf16[768,1024]{1,0:T(8,128)(2,1)} %input_ref.3) | copy-start | bytes 4718596
  0.0 24.4 %all-to-all-start = ((f32[8,32,768]{2,1,0:T(8,128)}), f32[8,32,768]{2,1,0:T(8,128)S(1)}, u32[]{:S(2)}, u32[]{:S(2)}) async-start(f32[8,32,768]{2,1,0:T(8,128)} %bitcast.9), calls=%async_computation | async-start | bytes 1572864 | tf_op jit(solution)/shard_map/all_to_all | solution.py:274
  24.4 1.6 %copy-start = (bf16[1024,1024]{1,0:T(8,128)(2,1)S(1)}, bf16[1024,1024]{1,0:T(8,128)(2,1)}, u32[]{:S(2)}) copy-start(bf16[1024,1024]{1,0:T(8,128)(2,1)} %first_ref.3) | copy-start | bytes 6291460
  26.0 1.6 %copy-start.2 = (bf16[1024,1024]{1,0:T(8,128)(2,1)S(1)}, bf16[1024,1024]{1,0:T(8,128)(2,1)}, u32[]{:S(2)}) copy-start(bf16[1024,1024]{1,0:T(8,128)(2,1)} %second_ref.3) | copy-start | bytes 6291460
  27.6 1.4 %copy-start.5 = (bf16[1024,768]{1,0:T(8,128)(2,1)S(1)}, bf16[1024,768]{1,0:T(8,128)(2,1)}, u32[]{:S(2)}) copy-start(bf16[1024,768]{1,0:T(8,128)(2,1)} %output_ref.3) | copy-start | bytes 4718596
  29.0 1.2 %copy-start.6 = (bf16[256,2048]{1,0:T(8,128)(2,1)S(1)}, bf16[256,2048]{1,0:T(8,128)(2,1)}, u32[]{:S(2)}) copy-start(bf16[256,2048]{1,0:T(8,128)(2,1)} %embed_ref.1) | copy-start | bytes 3145732
  30.2 1.1 %copy-start.7 = (f32[8,32,768]{2,1,0:T(8,128)S(1)}, f32[8,32,768]{2,1,0:T(8,128)}, u32[]{:S(2)}) copy-start(f32[8,32,768]{2,1,0:T(8,128)} %start_ref.1) | copy-start | bytes 2359300
  31.4 0.7 copy-start.8
  32.1 10.3 %copy-start.1 = (bf16[1024,1024]{1,0:T(8,128)(2,1)S(1)}, bf16[1024,1024]{1,0:T(8,128)(2,1)}, u32[]{:S(2)}) copy-start(bf16[1024,1024]{1,0:T(8,128)(2,1)} %first_ref.3) | copy-start | bytes 6291460
  32.1 10.3 %copy-start.3 = (bf16[1024,1024]{1,0:T(8,128)(2,1)S(1)}, bf16[1024,1024]{1,0:T(8,128)(2,1)}, u32[]{:S(2)}) copy-start(bf16[1024,1024]{1,0:T(8,128)(2,1)} %second_ref.3) | copy-start | bytes 6291460
  38.0 4.4 %collective-permute-start = (f32[32,768]{1,0:T(8,128)S(1)}, f32[32,768]{1,0:T(8,128)S(1)}, u32[]{:S(2)}, u32[]{:S(2)}) collective-permute-start(f32[32,768]{1,0:T(8,128)S(1)} %get-tuple-element.13), channel_id=1, source_target_pairs={{0,8},{1,9},{2,10},{3,11},{4,12},{5,13},{6,14},{7,15},{16,24},{17,... | collective-permute-start | bytes 294920 | tf_op jit(solution)/shard_map/ppermute | solution.py:243
  47.9 7.5 %collective-permute-start.1 = (f32[32,768]{1,0:T(8,128)S(1)}, f32[32,768]{1,0:T(8,128)S(1)}, u32[]{:S(2)}, u32[]{:S(2)}) collective-permute-start(f32[32,768]{1,0:T(8,128)S(1)} %get-tuple-element.18), channel_id=1, source_target_pairs={{0,8},{1,9},{2,10},{3,11},{4,12},{5,13},{6,14},{7,15},{16,24},{17,... | collective-permute-start | bytes 294920 | tf_op jit(solution)/shard_map/ppermute | solution.py:243

commit v3 on v2

--- a/solution.py
+++ b/solution.py
@@ -15,6 +15,7 @@
 LANES = 128
 CHUNK = 256
 COEFS = 5
+SPLIT = 2
 
 
 def noise_table():
@@ -60,26 +61,34 @@
     return jnp.dot(left, right, preferred_element_type=jnp.float32)
 
 
-def network(times, rows_ref, scale_ref, shift_ref, weights, entry_ref, hidden_ref, one_ref, two_ref, eps_ref):
-    input_weight, first_weight, second_weight, output_weight = weights
+def first_stage(times, rows_ref, scale_ref, shift_ref, input_weight, copies, next_copies, entry_ref, one_ref):
     features, channels = input_weight.shape
-    size = channels // GROUPS
     flat = jnp.concatenate([rows_ref[block] for block in range(features // LANES)], axis=1)
     flat = flat.astype(jnp.bfloat16)
+    wait_all(copies)
+    for parts in next_copies:
+        start_all(parts)
     for first in range(0, channels, CHUNK):
         columns = slice(first, first + CHUNK)
         entry_ref[:, columns] = dot(flat, input_weight[:, columns])
-        norm_silu(entry_ref, one_ref, first, times, size, scale_ref, shift_ref)
+        norm_silu(entry_ref, one_ref, first, times, channels // GROUPS, scale_ref, shift_ref)
+
+
+def later_stages(times, weights, copies, add_entry, hidden_ref, one_ref, two_ref, eps_ref):
+    first_weight, second_weight, output_weight = weights
+    channels, features = output_weight.shape
+    size = channels // GROUPS
+    wait_all(copies[0])
     for first in range(0, channels, CHUNK):
         columns = slice(first, first + CHUNK)
         hidden_ref[:, columns] = dot(one_ref[...], first_weight[:, columns])
         norm_silu(hidden_ref, two_ref, first, times, size, None, None)
+    wait_all(copies[1])
     for first in range(0, channels, CHUNK):
         columns = slice(first, first + CHUNK)
-        hidden_ref[:, columns] = entry_ref[:, columns] + dot(
-            two_ref[...], second_weight[:, columns]
-        )
+        hidden_ref[:, columns] = add_entry(columns, dot(two_ref[...], second_weight[:, columns]))
         norm_silu(hidden_ref, one_ref, first, times, size, None, None)
+    wait_all(copies[2])
     for first in range(0, features, CHUNK):
         part = dot(one_ref[...], output_weight[:, first : first + CHUNK])
         for lane in range(0, CHUNK, LANES):
@@ -104,6 +113,32 @@
     return clean_part * clean + state_part * state + sigma * noise
 
 
+def plan_copies(sources, targets, sems):
+    copies = []
+    for index, (source, target) in enumerate(zip(sources, targets)):
+        step = source.shape[0] // SPLIT
+        parts = [
+            pltpu.make_async_copy(
+                source.at[pl.ds(part * step, step)],
+                target.at[pl.ds(part * step, step)],
+                sems.at[index * SPLIT + part],
+            )
+            for part in range(SPLIT)
+        ]
+        copies.append(parts)
+    return copies
+
+
+def start_all(parts):
+    for part in parts:
+        part.start()
+
+
+def wait_all(parts):
+    for part in parts:
+        part.wait()
+
+
 def spread_rows(rows_ref, step, stride, values):
     patches, features = values.shape
     for block in range(features // LANES):
@@ -111,39 +146,86 @@
         rows_ref[block, pl.ds(step, patches, stride), :] = part
 
 
+def prepare_kernel(
+    width,
+    start_hbm,
+    input_hbm,
+    gaps_ref,
+    opening_ref,
+    own_ref,
+    entry_ref,
+    norm_ref,
+    part_ref,
+    input_ref,
+    own_sem,
+    sems,
+):
+    place = lax.axis_index(TIME)
+    own_copy = pltpu.make_async_copy(start_hbm.at[lax.rem(place, width)], own_ref, own_sem)
+    own_copy.start()
+    (copies,) = plan_copies((input_hbm,), (input_ref,), sems)
+    start_all(copies)
+    later = lax.broadcasted_iota(jnp.int32, part_ref.shape, 1) > place
+    opening = jnp.where(place == 0, opening_ref[0], 0)
+    part_ref[...] = opening - jnp.where(later, gaps_ref[0], 0)
+    own_copy.wait()
+    patches = own_ref.shape[0]
+    channels = input_ref.shape[1]
+    size = channels // GROUPS
+    flat = own_ref[...].astype(jnp.bfloat16)
+    wait_all(copies)
+    for first in range(0, channels, CHUNK):
+        columns = slice(first, first + CHUNK)
+        entry_ref[:, columns] = dot(flat, input_ref[:, columns])
+        for lane in range(first, first + CHUNK, LANES):
+            columns = slice(lane, lane + LANES)
+            values = entry_ref[:, columns]
+
+            def mean(part):
+                sums = jnp.sum(part, axis=0, keepdims=True)
+                sums = jnp.broadcast_to(sums, (width, LANES))
+                return group_mean(sums, size, patches * size)[:1]
+
+            offset = values - mean(values)
+            norm_ref[:, columns] = offset * lax.rsqrt(mean(offset * offset) + 1e-05)
+
+
 def first_kernel(
     width,
-    start_ref,
+    own_ref,
+    entry_ref,
+    norm_ref,
     noise_ref,
     marks_ref,
     table_ref,
-    input_ref,
-    embed_ref,
-    first_ref,
-    second_ref,
-    output_ref,
+    embed_hbm,
+    first_hbm,
+    second_hbm,
+    output_hbm,
     state_ref,
     total_ref,
     scale_ref,
     shift_ref,
     coef_ref,
-    own_ref,
-    noise_buf,
-    rows_ref,
-    entry_ref,
     hidden_ref,
     one_ref,
     two_ref,
     eps_ref,
+    embed_ref,
+    first_ref,
+    second_ref,
+    output_ref,
     sems,
 ):
+    embed_copies, *copies = plan_copies(
+        (embed_hbm, first_hbm, second_hbm, output_hbm),
+        (embed_ref, first_ref, second_ref, output_ref),
+        sems,
+    )
+    start_all(embed_copies)
+    start_all(copies[0])
     place = lax.axis_index(TIME)
     image = lax.rem(place, width)
-    own_copy = pltpu.make_async_copy(start_ref.at[image], own_ref, sems.at[0])
-    own_copy.start()
-    noise_copy = pltpu.make_async_copy(noise_ref, noise_buf, sems.at[1])
-    noise_copy.start()
-
     patches, features = own_ref.shape
     lane = lax.broadcasted_iota(jnp.int32, (width, marks_ref.shape[1]), 1)
     time = lax.broadcasted_iota(jnp.int32, lane.shape, 0)
@@ -162,22 +244,30 @@
     half = embed_ref.shape[0] // 2
     order = lax.broadcasted_iota(jnp.int32, (1, half), 1).astype(jnp.float32)
     angles = now_mark * jnp.exp(-math.log(10000.0) * order / half)
-    channels = input_ref.shape[1]
+    channels = norm_ref.shape[1]
     cosine = jnp.cos(angles).astype(jnp.bfloat16)
     sine = jnp.sin(angles).astype(jnp.bfloat16)
     both = jnp.concatenate([cosine, sine], axis=1)
+    wait_all(embed_copies)
+    start_all(copies[1])
+    start_all(copies[2])
     scale_ref[...] = dot(both, embed_ref[:, :channels])
     shift_ref[...] = dot(both, embed_ref[:, channels:])
 
-    own_copy.wait()
-    own = own_ref[...]
-    for step in range(width):
-        spread_rows(rows_ref, step, width, own)
-    weights = (input_ref, first_ref, second_ref, output_ref)
-    network(
-        width, rows_ref, scale_ref, shift_ref, weights, entry_ref, hidden_ref, one_ref, two_ref, eps_ref
-    )
-    noise_copy.wait()
+    for lane in range(0, channels, LANES):
+        columns = slice(lane, lane + LANES)
+        gain = 0.5 * (1.0 + scale_ref[:, columns])
+        lift = 0.5 * shift_ref[:, columns]
+        half = norm_ref[:, columns][:, None, :] * gain[None] + lift[None]
+        act = half * jnp.tanh(half) + half
+        one_ref[:, columns] = act.reshape(patches * width, LANES).astype(jnp.bfloat16)
+
+    def add_entry(columns, part):
+        entry = entry_ref[:, columns]
+        return (part.reshape(patches, width, -1) + entry[:, None, :]).reshape(part.shape)
+
+    weights = (first_ref, second_ref, output_ref)
+    later_stages(width, weights, copies, add_entry, hidden_ref, one_ref, two_ref, eps_ref)
     for block in range(features // LANES):
         columns = slice(block * LANES, (block + 1) * LANES)
         base = own_ref[:, columns]
@@ -186,7 +276,7 @@
             eps = eps_ref[block, pl.ds(step, patches, width), :]
             row = [coef_ref[index, step : step + 1, :] for index in range(COEFS)]
             state_ref[step, :, columns] = base if running is None else base + running
-            change = drift(base, eps, noise_buf[step, :, columns], row)
+            change = drift(base, eps, noise_ref[step, :, columns], row)
             running = change if running is None else running + change
         total_ref[:, columns] = running
 
@@ -200,30 +290,35 @@
     shift_ref,
     coef_ref,
     input_ref,
-    first_ref,
-    second_ref,
-    output_ref,
+    first_hbm,
+    second_hbm,
+    output_hbm,
     sum_ref,
     total_ref,
-    noise_buf,
     rows_ref,
     entry_ref,
     hidden_ref,
     one_ref,
     two_ref,
     eps_ref,
+    first_ref,
+    second_ref,
+    output_ref,
     sems,
 ):
-    noise_copy = pltpu.make_async_copy(noise_ref, noise_buf, sems.at[0])
-    noise_copy.start()
+    weights = (first_ref, second_ref, output_ref)
+    copies = plan_copies((first_hbm, second_hbm, output_hbm), weights, sems)
     patches, features = earlier_ref.shape
     for step in range(width):
         spread_rows(rows_ref, step, width, state_ref[step] + earlier_ref[...])
-    weights = (input_ref, first_ref, second_ref, output_ref)
-    network(
-        width, rows_ref, scale_ref, shift_ref, weights, entry_ref, hidden_ref, one_ref, two_ref, eps_ref
-    )
-    noise_copy.wait()
+    first_stage(
+        width, rows_ref, scale_ref, shift_ref, input_ref, (), copies, entry_ref, one_ref
+    )
+
+    def add_entry(columns, part):
+        return entry_ref[:, columns] + part
+
+    later_stages(width, weights, copies, add_entry, hidden_ref, one_ref, two_ref, eps_ref)
     for block in range(features // LANES):
         columns = slice(block * LANES, (block + 1) * LANES)
         own = state_ref[0, :, columns]
@@ -232,7 +327,7 @@
             eps = eps_ref[block, pl.ds(step, patches, width), :]
             row = [coef_ref[index, step : step + 1, :] for index in range(COEFS)]
             state = state_ref[step, :, columns] + earlier_ref[:, columns]
-            change = drift(state, eps, noise_buf[step, :, columns], row)
+            change = drift(state, eps, noise_ref[step, :, columns], row)
             running = change if running is None else running + change
             sum_ref[step, :, columns] = own + running
         total_ref[:, columns] = running
@@ -268,34 +363,51 @@
     channels = input_weight.shape[1]
     assert count % width == 0 and width % 8 == 0
     groups = [list(range(first, first + width)) for first in range(0, count, width)]
-    place = lax.axis_index(TIME)
-
     def exchange(values):
         return lax.all_to_all(values, TIME, 0, 0, axis_index_groups=groups, tiled=True)
 
     noise = exchange(noise_draws[0])
     marks_length = -(-(count + 1) // LANES) * LANES
-    later = jnp.arange(marks_length, dtype=jnp.int32) > place
-    opening = jnp.where(place == 0, window_start[0], 0)
-    marks = lax.psum(opening - jnp.where(later, step_gaps[0], 0), TIME)[None]
 
     def shape(*dims):
         return jax.ShapeDtypeStruct(dims, jnp.float32)
 
     vmem = pl.BlockSpec(memory_space=pltpu.VMEM)
-    anywhere = pl.BlockSpec(memory_space=pl.ANY)
+    hbm = pl.BlockSpec(memory_space=pltpu.HBM)
     rows = width * patches
-    work = [
-        pltpu.VMEM((width, patches, features), jnp.float32),
-        pltpu.VMEM((features // LANES, rows, LANES), jnp.float32),
-        pltpu.VMEM((rows, channels), jnp.float32),
-        pltpu.VMEM((rows, channels), jnp.float32),
-        pltpu.VMEM((rows, channels), jnp.bfloat16),
-        pltpu.VMEM((rows, channels), jnp.bfloat16),
-        pltpu.VMEM((features // LANES, rows, LANES), jnp.float32),
-        pltpu.SemaphoreType.DMA((2,)),
-    ]
-    params = pltpu.CompilerParams(vmem_limit_bytes=24 * 2**20)
+    blocked = pltpu.VMEM((features // LANES, rows, LANES), jnp.float32)
+    wide = pltpu.VMEM((rows, channels), jnp.float32)
+    act = pltpu.VMEM((rows, channels), jnp.bfloat16)
+
+    def holder(weight):
+        return pltpu.VMEM(weight.shape, weight.dtype)
+
+    later = (first_weight, second_weight, output_weight)
+    later_weights = [holder(weight) for weight in later]
+
+    def limit(kib):
+        return pltpu.CompilerParams(vmem_limit_bytes=kib * 1024)
+
+    smem = pl.BlockSpec(memory_space=pltpu.SMEM)
+    own, entry, norm, part = pl.pallas_call(
+        functools.partial(prepare_kernel, width),
+        out_shape=(
+            shape(patches, features),
+            shape(patches, channels),
+            shape(patches, channels),
+            jax.ShapeDtypeStruct((1, marks_length), jnp.int32),
+        ),
+        in_specs=[hbm] * 2 + [smem] * 2,
+        out_specs=(vmem,) * 4,
+        scratch_shapes=[
+            holder(input_weight),
+            pltpu.SemaphoreType.DMA,
+            pltpu.SemaphoreType.DMA((SPLIT,)),
+        ],
+        compiler_params=limit(54800),
+        name="prepare",
+    )(start_state, input_weight, step_gaps, window_start)
+    marks = lax.psum(part, TIME)
     states, total, scale, shift, coefs = pl.pallas_call(
         functools.partial(first_kernel, width),
         out_shape=(
@@ -305,17 +417,19 @@
             shape(width, channels),
             shape(COEFS, width, LANES),
         ),
-        in_specs=[anywhere, anywhere] + [vmem] * 7,
+        in_specs=[vmem] * 6 + [hbm] * 4,
         out_specs=(vmem,) * 5,
-        scratch_shapes=[pltpu.VMEM((patches, features), jnp.float32)] + work,
-        compiler_params=params,
+        scratch_shapes=[wide, act, act, blocked, holder(embed_weight), *later_weights]
+        + [pltpu.SemaphoreType.DMA((4 * SPLIT,))],
+        compiler_params=limit(52500),
         name="first",
     )(
-        start_state,
+        own,
+        entry,
+        norm,
         noise,
         marks,
         jnp.asarray(noise_table()),
-        input_weight,
         embed_weight,
         first_weight,
         second_weight,
@@ -324,10 +438,12 @@
     sums, total = pl.pallas_call(
         functools.partial(second_kernel, width),
         out_shape=(shape(width, patches, features), shape(patches, features)),
-        in_specs=[vmem, vmem, anywhere] + [vmem] * 7,
+        in_specs=[vmem] * 7 + [hbm] * 3,
         out_specs=(vmem,) * 2,
-        scratch_shapes=work,
-        compiler_params=params,
+        scratch_shapes=[blocked, wide, wide, act, act, blocked]
+        + later_weights
+        + [pltpu.SemaphoreType.DMA((4 * SPLIT,))],
+        compiler_params=limit(50900),
         name="second",
     )(
         states,

time: 72.1 us -> 65.3 us (0.906)
  local copies, waits for them, and re-layouts: 8.52 us -> 0.89 us
  Pallas kernels: 11.4 us -> 14.9 us
  blocking collectives: 33 us -> 30.5 us
    unnamed x19 -> x5, local copies, waits for them, and re-layouts: 8.52 us -> 0.89 us
    pallas_call x0 -> x1, Pallas kernels: none -> 2.51 us  [shards(): pl.pallas_call(functools.partial(prepare_kernel, width), out_shape=(shape...]
    psum x1, blocking collectives: 17.7 us -> 15.2 us  [shards(): marks = lax.psum(part, TIME)]
  transfers between devices with their start and end apart: 3 -> 3, of which waited for: 2 -> 2; matrix products, arithmetic and copies ran while one was open for 0% -> 0% of each run, Pallas kernels for 0% -> 4%
where the time goes in v3:
time: 65.3 us; the launch traced here: 65 us
  blocking collectives  30.5 us (47%)
  Pallas kernels  14.9 us (23%)
  starting transfers between devices  12.9 us (20%)
  waiting for transfers between devices  4.38 us (7%)
  between operations  1.36 us (2%)
  local copies, waits for them, and re-layouts  0.89 us (1%)
    all_to_all x1, blocking collectives, exchange(): lax.all_to_all(values, TIME, 0, 0, axis_index_groups=groups, tiled=True)  15.3 us
    psum x1, blocking collectives, shards(): marks = lax.psum(part, TIME)  15.2 us
    ppermute x2, starting transfers between devices, shift_blocks(): return lax.ppermute(part, TIME, pairs)  7.52 us
    pallas_call x1, Pallas kernels, shards(): pl.pallas_call(functools.partial(first_kernel, width), out_shape=(shape(w...  6.42 us
    pallas_call x1, Pallas kernels, shards(): pl.pallas_call(functools.partial(second_kernel, width), out_shape=(shape(...  6.01 us
    all_to_all x1, starting transfers between devices, exchange(): lax.all_to_all(values, TIME, 0, 0, axis_index_groups=groups, tiled=True)  5.42 us
    ppermute x2, waiting for transfers between devices, shift_blocks(): return lax.ppermute(part, TIME, pairs)  4.38 us
    pallas_call x1, Pallas kernels, shards(): pl.pallas_call(functools.partial(prepare_kernel, width), out_shape=(shape...  2.51 us
  transfers between devices with their start and end apart: 3, of which 2 were waited for; matrix products, arithmetic and copies ran while one was open for 0% of the time, Pallas kernels for 4%

profile of v3, /device:TPU:0, one launch (start us, length us, event | category | flops | bytes accessed | tf_op | source)
XLA Modules:
  0.0 65.0 jit_solution(10352059682926405503)
XLA Ops:
  0.0 0.0 copy-start.1
  0.0 5.4 %all-to-all-start = ((f32[8,32,768]{2,1,0:T(8,128)}), f32[8,32,768]{2,1,0:T(8,128)S(1)}, u32[]{:S(2)}, u32[]{:S(2)}) async-start(f32[8,32,768]{2,1,0:T(8,128)} %bitcast.3), calls=%async_computation | async-start | bytes 1572864 | tf_op jit(solution)/shard_map/all_to_all | solution.py:367
  6.7 2.5 %prepare.1 = (f32[32,768]{1,0:T(8,128)S(1)}, f32[32,1024]{1,0:T(8,128)S(1)}, f32[32,1024]{1,0:T(8,128)S(1)}, s32[1,128]{1,0:T(1,128)S(1)}) custom-call(f32[8,32,768]{2,1,0:T(8,128)} %start_hbm.1, bf16[768,1024]{1,0:T(8,128)(2,1)} %input_ref.1, s32[1]{0:T(128)S(6)} %copy.12.gaps_ref, s32[1]{0:T(128)S(6)} %copy.13.opening_ref), custom_call_target="tpu_custom_call" | custom-call | tf_op jit(solution)/shard_map/prepare/pallas_call | solution.py:392
  9.2 15.2 %psum.7.marks_ref = s32[1,128]{1,0:T(1,128)S(1)} all-reduce(s32[1,128]{1,0:T(1,128)S(1)} %get-tuple-element.19), channel_id=1, replica_groups=mesh['groups'=2,'steps'=8,'inner'=2] {'steps','inner'}, use_global_device_ids=true, to_apply=%region_0.0 | all-reduce | flops 128 | bytes 1024 | tf_op jit(solution)/shard_map/psum | solution.py:410
  24.4 0.0 all-to-all-done.noise_ref
  24.4 0.0 copy-done.1
  24.4 0.0 copy-start
  24.4 6.4 %first.1 = (f32[8,32,768]{2,1,0:T(8,128)S(1)}, f32[32,768]{1,0:T(8,128)S(1)}, f32[8,1024]{1,0:T(8,128)S(1)}, f32[8,1024]{1,0:T(8,128)S(1)}, f32[5,8,128]{2,1,0:T(8,128)S(1)}) custom-call(f32[32,768]{1,0:T(8,128)S(1)} %get-tuple-element.16.own_ref, f32[32,1024]{1,0:T(8,128)S(1)} %get-tuple-element.17.entry_ref, f32[32,1024]{1,0:T(8,128)S(1)} %get-tuple-element.18.norm_ref, ...), custom_call_target="tpu_custom_call" | custom-call | tf_op jit(solution)/shard_map/first/pallas_call | solution.py:411
  30.9 2.2 %collective-permute-start = (f32[32,768]{1,0:T(8,128)S(1)}, f32[32,768]{1,0:T(8,128)S(1)}, u32[]{:S(2)}, u32[]{:S(2)}) collective-permute-start(f32[32,768]{1,0:T(8,128)S(1)} %get-tuple-element.21), channel_id=1, source_target_pairs={{0,8},{1,9},{2,10},{3,11},{4,12},{5,13},{6,14},{7,15},{16,24},{17,... | collective-permute-start | bytes 294920 | tf_op jit(solution)/shard_map/ppermute | solution.py:338
  33.1 2.2 %collective-permute-done.earlier_ref = f32[32,768]{1,0:T(8,128)S(1)} collective-permute-done((f32[32,768]{1,0:T(8,128)S(1)}, f32[32,768]{1,0:T(8,128)S(1)}, u32[]{:S(2)}, u32[]{:S(2)}) %collective-permute-start) | collective-permute-done | bytes 98336 | tf_op jit(solution)/shard_map/ppermute | solution.py:338
  35.3 0.0 copy-done
  35.3 6.0 %second.1 = (f32[8,32,768]{2,1,0:T(8,128)S(1)}, f32[32,768]{1,0:T(8,128)S(1)}) custom-call(f32[8,32,768]{2,1,0:T(8,128)S(1)} %get-tuple-element.20.state_ref, f32[32,768]{1,0:T(8,128)S(1)} %collective-permute-done.earlier_ref, f32[8,32,768]{2,1,0:T(8,128)S(1)} %all-to-all-done.noise_ref, f32[8,1024]{1,0:T(8,128)S(1)} %get-tuple-element.22.scale_ref, ...), custom_call_target="tpu_custom_call" | custom-call | tf_op jit(solution)/shard_map/second/pallas_call | solution.py:438
  41.3 5.3 %collective-permute-start.1 = (f32[32,768]{1,0:T(8,128)S(1)}, f32[32,768]{1,0:T(8,128)S(1)}, u32[]{:S(2)}, u32[]{:S(2)}) collective-permute-start(f32[32,768]{1,0:T(8,128)S(1)} %get-tuple-element.26), channel_id=1, source_target_pairs={{0,8},{1,9},{2,10},{3,11},{4,12},{5,13},{6,14},{7,15},{16,24},{17,... | collective-permute-start | bytes 294920 | tf_op jit(solution)/shard_map/ppermute | solution.py:338
  46.6 2.2 %collective-permute-done.1 = f32[32,768]{1,0:T(8,128)S(1)} collective-permute-done((f32[32,768]{1,0:T(8,128)S(1)}, f32[32,768]{1,0:T(8,128)S(1)}, u32[]{:S(2)}, u32[]{:S(2)}) %collective-permute-start.1) | collective-permute-done | bytes 98336 | tf_op jit(solution)/shard_map/ppermute | solution.py:338
  48.8 0.1 broadcast_add_fusion
  48.9 15.3 %all_to_all.10 = f32[8,32,768]{2,1,0:T(8,128)S(1)} all-to-all(f32[8,32,768]{2,1,0:T(8,128)S(1)} %broadcast_add_fusion), channel_id=1, replica_groups={{0,1,2,3,4,5,6,7},{8,9,10,11,12,13,14,15},{16,17,18,19,20,21,22,23},{24..., dimensions={0} | all-to-all | bytes 1572864 | tf_op jit(solution)/shard_map/all_to_all | solution.py:367
  64.1 0.9 %copy.14 = f32[1,8,32,768]{3,2,1,0:T(8,128)} copy(f32[1,8,32,768]{3,2,1,0:T(8,128)S(1)} %bitcast.2) | data formatting | bytes 1572864
Async XLA Ops:
  0.0 24.4 %copy-start.1 = (f32[1,1024]{1,0:T(1,128)S(1)}, f32[1,1024]{1,0:T(1,128)}, u32[]{:S(2)}) copy-start(f32[1,1024]{1,0:T(1,128)} %constant.2.clone.table_ref) | copy-start | bytes 12292
  0.0 24.4 %all-to-all-start = ((f32[8,32,768]{2,1,0:T(8,128)}), f32[8,32,768]{2,1,0:T(8,128)S(1)}, u32[]{:S(2)}, u32[]{:S(2)}) async-start(f32[8,32,768]{2,1,0:T(8,128)} %bitcast.3), calls=%async_computation | async-start | bytes 1572864 | tf_op jit(solution)/shard_map/all_to_all | solution.py:367
  24.4 10.8 %copy-start = (bf16[768,1024]{1,0:T(8,128)(2,1)S(1)}, bf16[768,1024]{1,0:T(8,128)(2,1)}, u32[]{:S(2)}) copy-start(bf16[768,1024]{1,0:T(8,128)(2,1)} %input_ref.1) | copy-start | bytes 4718596
  30.9 4.4 %collective-permute-start = (f32[32,768]{1,0:T(8,128)S(1)}, f32[32,768]{1,0:T(8,128)S(1)}, u32[]{:S(2)}, u32[]{:S(2)}) collective-permute-start(f32[32,768]{1,0:T(8,128)S(1)} %get-tuple-element.21), channel_id=1, source_target_pairs={{0,8},{1,9},{2,10},{3,11},{4,12},{5,13},{6,14},{7,15},{16,24},{17,... | collective-permute-start | bytes 294920 | tf_op jit(solution)/shard_map/ppermute | solution.py:338
  41.3 7.5 %collective-permute-start.1 = (f32[32,768]{1,0:T(8,128)S(1)}, f32[32,768]{1,0:T(8,128)S(1)}, u32[]{:S(2)}, u32[]{:S(2)}) collective-permute-start(f32[32,768]{1,0:T(8,128)S(1)} %get-tuple-element.26), channel_id=1, source_target_pairs={{0,8},{1,9},{2,10},{3,11},{4,12},{5,13},{6,14},{7,15},{16,24},{17,... | collective-permute-start | bytes 294920 | tf_op jit(solution)/shard_map/ppermute | solution.py:338

commit v4 on v3

--- a/solution.py
+++ b/solution.py
@@ -281,6 +281,18 @@
         total_ref[:, columns] = running
 
 
+def early_kernel(width, *refs):
+    @pl.when(lax.axis_index(TIME) < width)
+    def _():
+        second_kernel(width, refs[0], None, *refs[1:])
+
+
+def late_kernel(width, sums_ref, *refs):
+    @pl.when(lax.axis_index(TIME) >= width)
+    def _():
+        second_kernel(width, *refs[:11], None, *refs[11:])
+
+
 def second_kernel(
     width,
     state_ref,
@@ -308,9 +320,14 @@
 ):
     weights = (first_ref, second_ref, output_ref)
     copies = plan_copies((first_hbm, second_hbm, output_hbm), weights, sems)
-    patches, features = earlier_ref.shape
+    _, patches, features = state_ref.shape
+
+    def state_of(step, columns):
+        state = state_ref[step, :, columns]
+        return state if earlier_ref is None else state + earlier_ref[:, columns]
+
     for step in range(width):
-        spread_rows(rows_ref, step, width, state_ref[step] + earlier_ref[...])
+        spread_rows(rows_ref, step, width, state_of(step, slice(None)))
     first_stage(
         width, rows_ref, scale_ref, shift_ref, input_ref, (), copies, entry_ref, one_ref
     )
@@ -326,11 +343,11 @@
         for step in range(width):
             eps = eps_ref[block, pl.ds(step, patches, width), :]
             row = [coef_ref[index, step : step + 1, :] for index in range(COEFS)]
-            state = state_ref[step, :, columns] + earlier_ref[:, columns]
-            change = drift(state, eps, noise_ref[step, :, columns], row)
+            change = drift(state_of(step, columns), eps, noise_ref[step, :, columns], row)
             running = change if running is None else running + change
             sum_ref[step, :, columns] = own + running
-        total_ref[:, columns] = running
+        if total_ref is not None:
+            total_ref[:, columns] = running
 
 
 def shift_blocks(part, count, width, blocks):
@@ -435,29 +452,48 @@
         second_weight,
         output_weight,
     )
+    scratch = [blocked, wide, wide, act, act, blocked, *later_weights]
+    scratch.append(pltpu.SemaphoreType.DMA((4 * SPLIT,)))
+    sums_shape = shape(width, patches, features)
+    total_shape = shape(patches, features)
+    common = (noise, scale, shift, coefs, input_weight, *later)
+    flops = 2 * rows * channels * (2 * features + 2 * channels)
+    cost = pl.CostEstimate(flops=flops, transcendentals=0, bytes_accessed=8 * 2**20)
+    if count != 2 * width:
+        sums, total = pl.pallas_call(
+            functools.partial(second_kernel, width),
+            out_shape=(sums_shape, total_shape),
+            in_specs=[vmem] * 7 + [hbm] * 3,
+            out_specs=(vmem,) * 2,
+            scratch_shapes=scratch,
+            compiler_params=limit(50900),
+            name="second",
+        )(states, earlier_blocks(total, count, width), *common)
+        return exchange(sums + earlier_blocks(total, count, width))[None]
+    earlier = earlier_blocks(total, count, width)
     sums, total = pl.pallas_call(
-        functools.partial(second_kernel, width),
-        out_shape=(shape(width, patches, features), shape(patches, features)),
-        in_specs=[vmem] * 7 + [hbm] * 3,
+        functools.partial(early_kernel, width),
+        out_shape=(sums_shape, total_shape),
+        in_specs=[vmem] * 6 + [hbm] * 3,
         out_specs=(vmem,) * 2,
-        scratch_shapes=[blocked, wide, wide, act, act, blocked]
-        + later_weights
-        + [pltpu.SemaphoreType.DMA((4 * SPLIT,))],
+        scratch_shapes=scratch,
+        cost_estimate=cost,
         compiler_params=limit(50900),
-        name="second",
-    )(
-        states,
-        earlier_blocks(total, count, width),
-        noise,
-        scale,
-        shift,
-        coefs,
-        input_weight,
-        first_weight,
-        second_weight,
-        output_weight,
-    )
-    return exchange(sums + earlier_blocks(total, count, width))[None]
+        name="early",
+    )(states, *common)
+    moved = earlier_blocks(total, count, width)
+    sums = pl.pallas_call(
+        functools.partial(late_kernel, width),
+        out_shape=sums_shape,
+        in_specs=[vmem] * 8 + [hbm] * 3,
+        out_specs=vmem,
+        scratch_shapes=scratch,
+        input_output_aliases={0: 0},
+        cost_estimate=cost,
+        compiler_params=limit(50900),
+        name="late",
+    )(sums, states, earlier, *common)
+    return exchange(sums + moved)[None]
 
 
 def solution(mesh):

time: 65.3 us -> 58.1 us (0.89)
  starting transfers between devices: 12.9 us -> 8.92 us
  waiting for transfers between devices: 4.38 us -> 1.91 us
  blocking collectives: 30.5 us -> 29.4 us
    ppermute x2, starting transfers between devices: 7.52 us -> 3.5 us  [shift_blocks(): return lax.ppermute(part, TIME, pairs)]
    ppermute x2, waiting for transfers between devices: 4.38 us -> 1.9 us  [shift_blocks(): return lax.ppermute(part, TIME, pairs)]
    all_to_all x1, blocking collectives: 15.3 us -> 14.2 us  [exchange(): lax.all_to_all(values, TIME, 0, 0, axis_index_groups=groups, tiled=True)]
    pallas_call x1 -> x2, Pallas kernels: 6.01 us -> 6.29 us  [the longest x1 6.02 us: shards(): pl.pallas_call(functools.partial(early_kernel, width), out_shape=(sums_sh...]
  transfers between devices with their start and end apart: 3 -> 3, of which waited for: 2 -> 1; matrix products, arithmetic and copies ran while one was open for 0% -> 0% of each run, Pallas kernels for 4% -> 15%
where the time goes in v4:
time: 58.1 us; the launch traced here: 57.8 us
  blocking collectives  29.4 us (51%)
  Pallas kernels  15.2 us (26%)
  starting transfers between devices  8.92 us (15%)
  waiting for transfers between devices  1.91 us (3%)
  between operations  1.38 us (2%)
  local copies, waits for them, and re-layouts  0.89 us (2%)
    psum x1, blocking collectives, shards(): marks = lax.psum(part, TIME)  15.2 us
    all_to_all x1, blocking collectives, exchange(): lax.all_to_all(values, TIME, 0, 0, axis_index_groups=groups, tiled=True)  14.2 us
    pallas_call x1, Pallas kernels, shards(): pl.pallas_call(functools.partial(first_kernel, width), out_shape=(shape(w...  6.43 us
    pallas_call x1, Pallas kernels, shards(): pl.pallas_call(functools.partial(early_kernel, width), out_shape=(sums_sh...  6.02 us
    all_to_all x1, starting transfers between devices, exchange(): lax.all_to_all(values, TIME, 0, 0, axis_index_groups=groups, tiled=True)  5.42 us
    ppermute x2, starting transfers between devices, shift_blocks(): return lax.ppermute(part, TIME, pairs)  3.5 us
    pallas_call x1, Pallas kernels, shards(): pl.pallas_call(functools.partial(prepare_kernel, width), out_shape=(shape...  2.51 us
    ppermute x2, waiting for transfers between devices, shift_blocks(): return lax.ppermute(part, TIME, pairs)  1.9 us
  transfers between devices with their start and end apart: 3, of which 1 were waited for; matrix products, arithmetic and copies ran while one was open for 0% of the time, Pallas kernels for 15%

profile of v4, /device:TPU:0, one launch (start us, length us, event | category | flops | bytes accessed | tf_op | source)
XLA Modules:
  0.0 57.8 jit_solution(3493427602664341058)
XLA Ops:
  0.0 0.0 copy-start.1
  0.0 5.4 %all-to-all-start = ((f32[8,32,768]{2,1,0:T(8,128)}), f32[8,32,768]{2,1,0:T(8,128)S(1)}, u32[]{:S(2)}, u32[]{:S(2)}) async-start(f32[8,32,768]{2,1,0:T(8,128)} %bitcast.3), calls=%async_computation | async-start | bytes 1572864 | tf_op jit(solution)/shard_map/all_to_all | solution.py:384
  6.7 2.5 %prepare.1 = (f32[32,768]{1,0:T(8,128)S(1)}, f32[32,1024]{1,0:T(8,128)S(1)}, f32[32,1024]{1,0:T(8,128)S(1)}, s32[1,128]{1,0:T(1,128)S(1)}) custom-call(f32[8,32,768]{2,1,0:T(8,128)} %start_hbm.1, bf16[768,1024]{1,0:T(8,128)(2,1)} %refs_6_.3, s32[1]{0:T(128)S(6)} %copy.14.gaps_ref, s32[1]{0:T(128)S(6)} %copy.15.opening_ref), custom_call_target="tpu_custom_call" | custom-call | tf_op jit(solution)/shard_map/prepare/pallas_call | solution.py:409
  9.2 15.2 %psum.7.marks_ref = s32[1,128]{1,0:T(1,128)S(1)} all-reduce(s32[1,128]{1,0:T(1,128)S(1)} %get-tuple-element.19), channel_id=1, replica_groups=mesh['groups'=2,'steps'=8,'inner'=2] {'steps','inner'}, use_global_device_ids=true, to_apply=%region_0.0 | all-reduce | flops 128 | bytes 1024 | tf_op jit(solution)/shard_map/psum | solution.py:427
  24.4 0.0 all-to-all-done.noise_ref.refs_1_.refs_2_
  24.4 0.0 copy-done.1
  24.4 0.0 copy-start
  24.4 6.4 %first.1 = (f32[8,32,768]{2,1,0:T(8,128)S(1)}, f32[32,768]{1,0:T(8,128)S(1)}, f32[8,1024]{1,0:T(8,128)S(1)}, f32[8,1024]{1,0:T(8,128)S(1)}, f32[5,8,128]{2,1,0:T(8,128)S(1)}) custom-call(f32[32,768]{1,0:T(8,128)S(1)} %get-tuple-element.16.own_ref, f32[32,1024]{1,0:T(8,128)S(1)} %get-tuple-element.17.entry_ref, f32[32,1024]{1,0:T(8,128)S(1)} %get-tuple-element.18.norm_ref, ...), custom_call_target="tpu_custom_call" | custom-call | tf_op jit(solution)/shard_map/first/pallas_call | solution.py:428
  30.9 2.2 %collective-permute-start = (f32[32,768]{1,0:T(8,128)S(1)}, f32[32,768]{1,0:T(8,128)S(1)}, u32[]{:S(2)}, u32[]{:S(2)}) collective-permute-start(f32[32,768]{1,0:T(8,128)S(1)} %get-tuple-element.25), channel_id=1, source_target_pairs={{0,8},{1,9},{2,10},{3,11},{4,12},{5,13},{6,14},{7,15},{16,24},{17,... | collective-permute-start | bytes 294920 | tf_op jit(solution)/shard_map/ppermute | solution.py:355
  33.1 0.0 copy-done
  33.1 6.0 %early.1 = (f32[8,32,768]{2,1,0:T(8,128)S(1)}, f32[32,768]{1,0:T(8,128)S(1)}) custom-call(f32[8,32,768]{2,1,0:T(8,128)S(1)} %get-tuple-element.20.refs_0_, f32[8,32,768]{2,1,0:T(8,128)S(1)} %all-to-all-done.noise_ref.refs_1_.refs_2_, f32[8,1024]{1,0:T(8,128)S(1)} %get-tuple-element.21.refs_2_.refs_3_, f32[8,1024]{1,0:T(8,128)S(1)} %get-tuple-element.22.refs_3_.refs_4_, ...), custom_call_target="tpu_custom_call" | custom-call | flops 1879048192 | bytes 8388608 | tf_op jit(solution)/shard_map/early/pallas_call | solution.py:474
  39.1 1.3 %collective-permute-start.1 = (f32[32,768]{1,0:T(8,128)S(1)}, f32[32,768]{1,0:T(8,128)S(1)}, u32[]{:S(2)}, u32[]{:S(2)}) collective-permute-start(f32[32,768]{1,0:T(8,128)S(1)} %get-tuple-element.26), channel_id=1, source_target_pairs={{0,8},{1,9},{2,10},{3,11},{4,12},{5,13},{6,14},{7,15},{16,24},{17,... | collective-permute-start | bytes 294920 | tf_op jit(solution)/shard_map/ppermute | solution.py:355
  40.4 0.0 collective-permute-done.refs_1_
  40.4 0.3 late.1
  40.7 1.9 %collective-permute-done.1 = f32[32,768]{1,0:T(8,128)S(1)} collective-permute-done((f32[32,768]{1,0:T(8,128)S(1)}, f32[32,768]{1,0:T(8,128)S(1)}, u32[]{:S(2)}, u32[]{:S(2)}) %collective-permute-start.1) | collective-permute-done | bytes 98336 | tf_op jit(solution)/shard_map/ppermute | solution.py:355
  42.6 0.1 broadcast_add_fusion
  42.7 14.2 %all_to_all.10 = f32[8,32,768]{2,1,0:T(8,128)S(1)} all-to-all(f32[8,32,768]{2,1,0:T(8,128)S(1)} %broadcast_add_fusion), channel_id=1, replica_groups={{0,1,2,3,4,5,6,7},{8,9,10,11,12,13,14,15},{16,17,18,19,20,21,22,23},{24..., dimensions={0} | all-to-all | bytes 1572864 | tf_op jit(solution)/shard_map/all_to_all | solution.py:384
  56.9 0.9 %copy.16 = f32[1,8,32,768]{3,2,1,0:T(8,128)} copy(f32[1,8,32,768]{3,2,1,0:T(8,128)S(1)} %bitcast.2) | data formatting | bytes 1572864
Async XLA Ops:
  0.0 24.4 %copy-start.1 = (f32[1,1024]{1,0:T(1,128)S(1)}, f32[1,1024]{1,0:T(1,128)}, u32[]{:S(2)}) copy-start(f32[1,1024]{1,0:T(1,128)} %constant.2.clone.table_ref) | copy-start | bytes 12292
  0.0 24.4 %all-to-all-start = ((f32[8,32,768]{2,1,0:T(8,128)}), f32[8,32,768]{2,1,0:T(8,128)S(1)}, u32[]{:S(2)}, u32[]{:S(2)}) async-start(f32[8,32,768]{2,1,0:T(8,128)} %bitcast.3), calls=%async_computation | async-start | bytes 1572864 | tf_op jit(solution)/shard_map/all_to_all | solution.py:384
  24.4 8.7 %copy-start = (bf16[768,1024]{1,0:T(8,128)(2,1)S(1)}, bf16[768,1024]{1,0:T(8,128)(2,1)}, u32[]{:S(2)}) copy-start(bf16[768,1024]{1,0:T(8,128)(2,1)} %refs_6_.3) | copy-start | bytes 4718596
  30.9 9.6 %collective-permute-start = (f32[32,768]{1,0:T(8,128)S(1)}, f32[32,768]{1,0:T(8,128)S(1)}, u32[]{:S(2)}, u32[]{:S(2)}) collective-permute-start(f32[32,768]{1,0:T(8,128)S(1)} %get-tuple-element.25), channel_id=1, source_target_pairs={{0,8},{1,9},{2,10},{3,11},{4,12},{5,13},{6,14},{7,15},{16,24},{17,... | collective-permute-start | bytes 294920 | tf_op jit(solution)/shard_map/ppermute | solution.py:355
  39.1 3.5 %collective-permute-start.1 = (f32[32,768]{1,0:T(8,128)S(1)}, f32[32,768]{1,0:T(8,128)S(1)}, u32[]{:S(2)}, u32[]{:S(2)}) collective-permute-start(f32[32,768]{1,0:T(8,128)S(1)} %get-tuple-element.26), channel_id=1, source_target_pairs={{0,8},{1,9},{2,10},{3,11},{4,12},{5,13},{6,14},{7,15},{16,24},{17,... | collective-permute-start | bytes 294920 | tf_op jit(solution)/shard_map/ppermute | solution.py:355

commit v5 on v4

--- a/solution.py
+++ b/solution.py
@@ -15,7 +15,7 @@
 LANES = 128
 CHUNK = 256
 COEFS = 5
-SPLIT = 2
+SPLIT = 1
 
 
 def noise_table():
@@ -438,7 +438,7 @@
         out_specs=(vmem,) * 5,
         scratch_shapes=[wide, act, act, blocked, holder(embed_weight), *later_weights]
         + [pltpu.SemaphoreType.DMA((4 * SPLIT,))],
-        compiler_params=limit(52500),
+        compiler_params=limit(51300),
         name="first",
     )(
         own,

time: 58.1 us -> 57.8 us (level)
  no operation moved by 1% of the time
where the time goes in v5:
time: 57.8 us; the launch traced here: 57.5 us
  blocking collectives  29.3 us (51%)
  Pallas kernels  14.9 us (26%)
  starting transfers between devices  8.92 us (15%)
  waiting for transfers between devices  1.94 us (3%)
  between operations  1.39 us (2%)
  local copies, waits for them, and re-layouts  0.89 us (2%)
    psum x1, blocking collectives, shards(): marks = lax.psum(part, TIME)  15.1 us
    all_to_all x1, blocking collectives, exchange(): lax.all_to_all(values, TIME, 0, 0, axis_index_groups=groups, tiled=True)  14.2 us
    pallas_call x1, Pallas kernels, shards(): pl.pallas_call(functools.partial(first_kernel, width), out_shape=(shape(w...  6.18 us
    pallas_call x1, Pallas kernels, shards(): pl.pallas_call(functools.partial(early_kernel, width), out_shape=(sums_sh...  5.98 us
    all_to_all x1, starting transfers between devices, exchange(): lax.all_to_all(values, TIME, 0, 0, axis_index_groups=groups, tiled=True)  5.42 us
    ppermute x2, starting transfers between devices, shift_blocks(): return lax.ppermute(part, TIME, pairs)  3.5 us
    pallas_call x1, Pallas kernels, shards(): pl.pallas_call(functools.partial(prepare_kernel, width), out_shape=(shape...  2.54 us
    ppermute x2, waiting for transfers between devices, shift_blocks(): return lax.ppermute(part, TIME, pairs)  1.94 us
  transfers between devices with their start and end apart: 3, of which 1 were waited for; matrix products, arithmetic and copies ran while one was open for 0% of the time, Pallas kernels for 15%

profile of v5, /device:TPU:0, one launch (start us, length us, event | category | flops | bytes accessed | tf_op | source)
XLA Modules:
  0.0 57.5 jit_solution(14967424436215815672)
XLA Ops:
  0.0 0.0 copy-start.2
  0.0 0.0 copy-start.1
  0.0 5.4 %all-to-all-start = ((f32[8,32,768]{2,1,0:T(8,128)}), f32[8,32,768]{2,1,0:T(8,128)S(1)}, u32[]{:S(2)}, u32[]{:S(2)}) async-start(f32[8,32,768]{2,1,0:T(8,128)} %bitcast.3), calls=%async_computation | async-start | bytes 1572864 | tf_op jit(solution)/shard_map/all_to_all | solution.py:384
  6.7 2.5 %prepare.1 = (f32[32,768]{1,0:T(8,128)S(1)}, f32[32,1024]{1,0:T(8,128)S(1)}, f32[32,1024]{1,0:T(8,128)S(1)}, s32[1,128]{1,0:T(1,128)S(1)}) custom-call(f32[8,32,768]{2,1,0:T(8,128)} %start_hbm.1, bf16[768,1024]{1,0:T(8,128)(2,1)} %refs_6_.3, s32[1]{0:T(128)S(6)} %copy.14.gaps_ref, s32[1]{0:T(128)S(6)} %copy.15.opening_ref), custom_call_target="tpu_custom_call" | custom-call | tf_op jit(solution)/shard_map/prepare/pallas_call | solution.py:409
  9.3 15.1 %psum.7.marks_ref = s32[1,128]{1,0:T(1,128)S(1)} all-reduce(s32[1,128]{1,0:T(1,128)S(1)} %get-tuple-element.19), channel_id=1, replica_groups=mesh['groups'=2,'steps'=8,'inner'=2] {'steps','inner'}, use_global_device_ids=true, to_apply=%region_0.0 | all-reduce | flops 128 | bytes 1024 | tf_op jit(solution)/shard_map/psum | solution.py:427
  24.4 0.0 all-to-all-done.noise_ref.refs_1_.refs_2_
  24.4 0.0 copy-done.2
  24.4 0.0 copy-done.1
  24.4 0.0 copy-start
  24.4 6.2 %first.1 = (f32[8,32,768]{2,1,0:T(8,128)S(1)}, f32[32,768]{1,0:T(8,128)S(1)}, f32[8,1024]{1,0:T(8,128)S(1)}, f32[8,1024]{1,0:T(8,128)S(1)}, f32[5,8,128]{2,1,0:T(8,128)S(1)}) custom-call(f32[32,768]{1,0:T(8,128)S(1)} %get-tuple-element.16.own_ref, f32[32,1024]{1,0:T(8,128)S(1)} %get-tuple-element.17.entry_ref, f32[32,1024]{1,0:T(8,128)S(1)} %get-tuple-element.18.norm_ref, ...), custom_call_target="tpu_custom_call" | custom-call | tf_op jit(solution)/shard_map/first/pallas_call | solution.py:428
  30.6 2.2 %collective-permute-start = (f32[32,768]{1,0:T(8,128)S(1)}, f32[32,768]{1,0:T(8,128)S(1)}, u32[]{:S(2)}, u32[]{:S(2)}) collective-permute-start(f32[32,768]{1,0:T(8,128)S(1)} %get-tuple-element.25), channel_id=1, source_target_pairs={{0,8},{1,9},{2,10},{3,11},{4,12},{5,13},{6,14},{7,15},{16,24},{17,... | collective-permute-start | bytes 294920 | tf_op jit(solution)/shard_map/ppermute | solution.py:355
  32.8 0.0 copy-done
  32.8 6.0 %early.1 = (f32[8,32,768]{2,1,0:T(8,128)S(1)}, f32[32,768]{1,0:T(8,128)S(1)}) custom-call(f32[8,32,768]{2,1,0:T(8,128)S(1)} %get-tuple-element.20.refs_0_, f32[8,32,768]{2,1,0:T(8,128)S(1)} %all-to-all-done.noise_ref.refs_1_.refs_2_, f32[8,1024]{1,0:T(8,128)S(1)} %get-tuple-element.21.refs_2_.refs_3_, f32[8,1024]{1,0:T(8,128)S(1)} %get-tuple-element.22.refs_3_.refs_4_, ...), custom_call_target="tpu_custom_call" | custom-call | flops 1879048192 | bytes 8388608 | tf_op jit(solution)/shard_map/early/pallas_call | solution.py:474
  38.8 1.3 %collective-permute-start.1 = (f32[32,768]{1,0:T(8,128)S(1)}, f32[32,768]{1,0:T(8,128)S(1)}, u32[]{:S(2)}, u32[]{:S(2)}) collective-permute-start(f32[32,768]{1,0:T(8,128)S(1)} %get-tuple-element.26), channel_id=1, source_target_pairs={{0,8},{1,9},{2,10},{3,11},{4,12},{5,13},{6,14},{7,15},{16,24},{17,... | collective-permute-start | bytes 294920 | tf_op jit(solution)/shard_map/ppermute | solution.py:355
  40.1 0.0 collective-permute-done.refs_1_
  40.2 0.2 late.1
  40.4 1.9 %collective-permute-done.1 = f32[32,768]{1,0:T(8,128)S(1)} collective-permute-done((f32[32,768]{1,0:T(8,128)S(1)}, f32[32,768]{1,0:T(8,128)S(1)}, u32[]{:S(2)}, u32[]{:S(2)}) %collective-permute-start.1) | collective-permute-done | bytes 98336 | tf_op jit(solution)/shard_map/ppermute | solution.py:355
  42.3 0.1 broadcast_add_fusion
  42.4 14.2 %all_to_all.10 = f32[8,32,768]{2,1,0:T(8,128)S(1)} all-to-all(f32[8,32,768]{2,1,0:T(8,128)S(1)} %broadcast_add_fusion), channel_id=1, replica_groups={{0,1,2,3,4,5,6,7},{8,9,10,11,12,13,14,15},{16,17,18,19,20,21,22,23},{24..., dimensions={0} | all-to-all | bytes 1572864 | tf_op jit(solution)/shard_map/all_to_all | solution.py:384
  56.6 0.9 %copy.16 = f32[1,8,32,768]{3,2,1,0:T(8,128)} copy(f32[1,8,32,768]{3,2,1,0:T(8,128)S(1)} %bitcast.2) | data formatting | bytes 1572864
Async XLA Ops:
  0.0 24.4 %copy-start.2 = (f32[1,1024]{1,0:T(1,128)S(1)}, f32[1,1024]{1,0:T(1,128)}, u32[]{:S(2)}) copy-start(f32[1,1024]{1,0:T(1,128)} %constant.2.clone.table_ref) | copy-start | bytes 12292
  0.0 24.4 %copy-start.1 = (bf16[256,2048]{1,0:T(8,128)(2,1)S(1)}, bf16[256,2048]{1,0:T(8,128)(2,1)}, u32[]{:S(2)}) copy-start(bf16[256,2048]{1,0:T(8,128)(2,1)} %embed_hbm.1) | copy-start | bytes 3145732
  0.0 24.4 %all-to-all-start = ((f32[8,32,768]{2,1,0:T(8,128)}), f32[8,32,768]{2,1,0:T(8,128)S(1)}, u32[]{:S(2)}, u32[]{:S(2)}) async-start(f32[8,32,768]{2,1,0:T(8,128)} %bitcast.3), calls=%async_computation | async-start | bytes 1572864 | tf_op jit(solution)/shard_map/all_to_all | solution.py:384
  24.4 8.4 %copy-start = (bf16[768,1024]{1,0:T(8,128)(2,1)S(1)}, bf16[768,1024]{1,0:T(8,128)(2,1)}, u32[]{:S(2)}) copy-start(bf16[768,1024]{1,0:T(8,128)(2,1)} %refs_6_.3) | copy-start | bytes 4718596
  30.6 9.5 %collective-permute-start = (f32[32,768]{1,0:T(8,128)S(1)}, f32[32,768]{1,0:T(8,128)S(1)}, u32[]{:S(2)}, u32[]{:S(2)}) collective-permute-start(f32[32,768]{1,0:T(8,128)S(1)} %get-tuple-element.25), channel_id=1, source_target_pairs={{0,8},{1,9},{2,10},{3,11},{4,12},{5,13},{6,14},{7,15},{16,24},{17,... | collective-permute-start | bytes 294920 | tf_op jit(solution)/shard_map/ppermute | solution.py:355
  38.8 3.5 %collective-permute-start.1 = (f32[32,768]{1,0:T(8,128)S(1)}, f32[32,768]{1,0:T(8,128)S(1)}, u32[]{:S(2)}, u32[]{:S(2)}) collective-permute-start(f32[32,768]{1,0:T(8,128)S(1)} %get-tuple-element.26), channel_id=1, source_target_pairs={{0,8},{1,9},{2,10},{3,11},{4,12},{5,13},{6,14},{7,15},{16,24},{17,... | collective-permute-start | bytes 294920 | tf_op jit(solution)/shard_map/ppermute | solution.py:355

commit v6 on v5

--- a/solution.py
+++ b/solution.py
@@ -320,6 +320,8 @@
 ):
     weights = (first_ref, second_ref, output_ref)
     copies = plan_copies((first_hbm, second_hbm, output_hbm), weights, sems)
+    for parts in copies:
+        start_all(parts)
     _, patches, features = state_ref.shape
 
     def state_of(step, columns):
@@ -329,7 +331,7 @@
     for step in range(width):
         spread_rows(rows_ref, step, width, state_of(step, slice(None)))
     first_stage(
-        width, rows_ref, scale_ref, shift_ref, input_ref, (), copies, entry_ref, one_ref
+        width, rows_ref, scale_ref, shift_ref, input_ref, (), (), entry_ref, one_ref
     )
 
     def add_entry(columns, part):

time: 57.8 us -> 57.8 us (level)
  no operation moved by 1% of the time
where the time goes in v6:
time: 57.8 us; the launch traced here: 57.5 us
  blocking collectives  29.3 us (51%)
  Pallas kernels  14.9 us (26%)
  starting transfers between devices  8.92 us (15%)
  waiting for transfers between devices  1.94 us (3%)
  between operations  1.39 us (2%)
  local copies, waits for them, and re-layouts  0.89 us (2%)
    psum x1, blocking collectives, shards(): marks = lax.psum(part, TIME)  15.1 us
    all_to_all x1, blocking collectives, exchange(): lax.all_to_all(values, TIME, 0, 0, axis_index_groups=groups, tiled=True)  14.2 us
    pallas_call x1, Pallas kernels, shards(): pl.pallas_call(functools.partial(first_kernel, width), out_shape=(shape(w...  6.18 us
    pallas_call x1, Pallas kernels, shards(): pl.pallas_call(functools.partial(early_kernel, width), out_shape=(sums_sh...  5.98 us
    all_to_all x1, starting transfers between devices, exchange(): lax.all_to_all(values, TIME, 0, 0, axis_index_groups=groups, tiled=True)  5.42 us
    ppermute x2, starting transfers between devices, shift_blocks(): return lax.ppermute(part, TIME, pairs)  3.5 us
    pallas_call x1, Pallas kernels, shards(): pl.pallas_call(functools.partial(prepare_kernel, width), out_shape=(shape...  2.54 us
    ppermute x2, waiting for transfers between devices, shift_blocks(): return lax.ppermute(part, TIME, pairs)  1.94 us
  transfers between devices with their start and end apart: 3, of which 1 were waited for; matrix products, arithmetic and copies ran while one was open for 0% of the time, Pallas kernels for 15%

profile of v6, /device:TPU:0, one launch (start us, length us, event | category | flops | bytes accessed | tf_op | source)
XLA Modules:
  0.0 57.5 jit_solution(14967424436215815672)
XLA Ops:
  0.0 0.0 copy-start.2
  0.0 0.0 copy-start.1
  0.0 5.4 %all-to-all-start = ((f32[8,32,768]{2,1,0:T(8,128)}), f32[8,32,768]{2,1,0:T(8,128)S(1)}, u32[]{:S(2)}, u32[]{:S(2)}) async-start(f32[8,32,768]{2,1,0:T(8,128)} %bitcast.3), calls=%async_computation | async-start | bytes 1572864 | tf_op jit(solution)/shard_map/all_to_all | solution.py:386
  6.7 2.5 %prepare.1 = (f32[32,768]{1,0:T(8,128)S(1)}, f32[32,1024]{1,0:T(8,128)S(1)}, f32[32,1024]{1,0:T(8,128)S(1)}, s32[1,128]{1,0:T(1,128)S(1)}) custom-call(f32[8,32,768]{2,1,0:T(8,128)} %start_hbm.1, bf16[768,1024]{1,0:T(8,128)(2,1)} %refs_6_.3, s32[1]{0:T(128)S(6)} %copy.14.gaps_ref, s32[1]{0:T(128)S(6)} %copy.15.opening_ref), custom_call_target="tpu_custom_call" | custom-call | tf_op jit(solution)/shard_map/prepare/pallas_call | solution.py:411
  9.3 15.1 %psum.7.marks_ref = s32[1,128]{1,0:T(1,128)S(1)} all-reduce(s32[1,128]{1,0:T(1,128)S(1)} %get-tuple-element.19), channel_id=1, replica_groups=mesh['groups'=2,'steps'=8,'inner'=2] {'steps','inner'}, use_global_device_ids=true, to_apply=%region_0.0 | all-reduce | flops 128 | bytes 1024 | tf_op jit(solution)/shard_map/psum | solution.py:429
  24.4 0.0 all-to-all-done.noise_ref.refs_1_.refs_2_
  24.4 0.0 copy-done.2
  24.4 0.0 copy-done.1
  24.4 0.0 copy-start
  24.4 6.2 %first.1 = (f32[8,32,768]{2,1,0:T(8,128)S(1)}, f32[32,768]{1,0:T(8,128)S(1)}, f32[8,1024]{1,0:T(8,128)S(1)}, f32[8,1024]{1,0:T(8,128)S(1)}, f32[5,8,128]{2,1,0:T(8,128)S(1)}) custom-call(f32[32,768]{1,0:T(8,128)S(1)} %get-tuple-element.16.own_ref, f32[32,1024]{1,0:T(8,128)S(1)} %get-tuple-element.17.entry_ref, f32[32,1024]{1,0:T(8,128)S(1)} %get-tuple-element.18.norm_ref, ...), custom_call_target="tpu_custom_call" | custom-call | tf_op jit(solution)/shard_map/first/pallas_call | solution.py:430
  30.6 2.2 %collective-permute-start = (f32[32,768]{1,0:T(8,128)S(1)}, f32[32,768]{1,0:T(8,128)S(1)}, u32[]{:S(2)}, u32[]{:S(2)}) collective-permute-start(f32[32,768]{1,0:T(8,128)S(1)} %get-tuple-element.25), channel_id=1, source_target_pairs={{0,8},{1,9},{2,10},{3,11},{4,12},{5,13},{6,14},{7,15},{16,24},{17,... | collective-permute-start | bytes 294920 | tf_op jit(solution)/shard_map/ppermute | solution.py:357
  32.8 0.0 copy-done
  32.8 6.0 %early.1 = (f32[8,32,768]{2,1,0:T(8,128)S(1)}, f32[32,768]{1,0:T(8,128)S(1)}) custom-call(f32[8,32,768]{2,1,0:T(8,128)S(1)} %get-tuple-element.20.refs_0_, f32[8,32,768]{2,1,0:T(8,128)S(1)} %all-to-all-done.noise_ref.refs_1_.refs_2_, f32[8,1024]{1,0:T(8,128)S(1)} %get-tuple-element.21.refs_2_.refs_3_, f32[8,1024]{1,0:T(8,128)S(1)} %get-tuple-element.22.refs_3_.refs_4_, ...), custom_call_target="tpu_custom_call" | custom-call | flops 1879048192 | bytes 8388608 | tf_op jit(solution)/shard_map/early/pallas_call | solution.py:476
  38.8 1.3 %collective-permute-start.1 = (f32[32,768]{1,0:T(8,128)S(1)}, f32[32,768]{1,0:T(8,128)S(1)}, u32[]{:S(2)}, u32[]{:S(2)}) collective-permute-start(f32[32,768]{1,0:T(8,128)S(1)} %get-tuple-element.26), channel_id=1, source_target_pairs={{0,8},{1,9},{2,10},{3,11},{4,12},{5,13},{6,14},{7,15},{16,24},{17,... | collective-permute-start | bytes 294920 | tf_op jit(solution)/shard_map/ppermute | solution.py:357
  40.1 0.0 collective-permute-done.refs_1_
  40.2 0.2 late.1
  40.4 1.9 %collective-permute-done.1 = f32[32,768]{1,0:T(8,128)S(1)} collective-permute-done((f32[32,768]{1,0:T(8,128)S(1)}, f32[32,768]{1,0:T(8,128)S(1)}, u32[]{:S(2)}, u32[]{:S(2)}) %collective-permute-start.1) | collective-permute-done | bytes 98336 | tf_op jit(solution)/shard_map/ppermute | solution.py:357
  42.3 0.1 broadcast_add_fusion
  42.4 14.2 %all_to_all.10 = f32[8,32,768]{2,1,0:T(8,128)S(1)} all-to-all(f32[8,32,768]{2,1,0:T(8,128)S(1)} %broadcast_add_fusion), channel_id=1, replica_groups={{0,1,2,3,4,5,6,7},{8,9,10,11,12,13,14,15},{16,17,18,19,20,21,22,23},{24..., dimensions={0} | all-to-all | bytes 1572864 | tf_op jit(solution)/shard_map/all_to_all | solution.py:386
  56.6 0.9 %copy.16 = f32[1,8,32,768]{3,2,1,0:T(8,128)} copy(f32[1,8,32,768]{3,2,1,0:T(8,128)S(1)} %bitcast.2) | data formatting | bytes 1572864
Async XLA Ops:
  0.0 24.4 %copy-start.2 = (f32[1,1024]{1,0:T(1,128)S(1)}, f32[1,1024]{1,0:T(1,128)}, u32[]{:S(2)}) copy-start(f32[1,1024]{1,0:T(1,128)} %constant.2.clone.table_ref) | copy-start | bytes 12292
  0.0 24.4 %copy-start.1 = (bf16[256,2048]{1,0:T(8,128)(2,1)S(1)}, bf16[256,2048]{1,0:T(8,128)(2,1)}, u32[]{:S(2)}) copy-start(bf16[256,2048]{1,0:T(8,128)(2,1)} %embed_hbm.1) | copy-start | bytes 3145732
  0.0 24.4 %all-to-all-start = ((f32[8,32,768]{2,1,0:T(8,128)}), f32[8,32,768]{2,1,0:T(8,128)S(1)}, u32[]{:S(2)}, u32[]{:S(2)}) async-start(f32[8,32,768]{2,1,0:T(8,128)} %bitcast.3), calls=%async_computation | async-start | bytes 1572864 | tf_op jit(solution)/shard_map/all_to_all | solution.py:386
  24.4 8.4 %copy-start = (bf16[768,1024]{1,0:T(8,128)(2,1)S(1)}, bf16[768,1024]{1,0:T(8,128)(2,1)}, u32[]{:S(2)}) copy-start(bf16[768,1024]{1,0:T(8,128)(2,1)} %refs_6_.3) | copy-start | bytes 4718596
  30.6 9.5 %collective-permute-start = (f32[32,768]{1,0:T(8,128)S(1)}, f32[32,768]{1,0:T(8,128)S(1)}, u32[]{:S(2)}, u32[]{:S(2)}) collective-permute-start(f32[32,768]{1,0:T(8,128)S(1)} %get-tuple-element.25), channel_id=1, source_target_pairs={{0,8},{1,9},{2,10},{3,11},{4,12},{5,13},{6,14},{7,15},{16,24},{17,... | collective-permute-start | bytes 294920 | tf_op jit(solution)/shard_map/ppermute | solution.py:357
  38.8 3.5 %collective-permute-start.1 = (f32[32,768]{1,0:T(8,128)S(1)}, f32[32,768]{1,0:T(8,128)S(1)}, u32[]{:S(2)}, u32[]{:S(2)}) collective-permute-start(f32[32,768]{1,0:T(8,128)S(1)} %get-tuple-element.26), channel_id=1, source_target_pairs={{0,8},{1,9},{2,10},{3,11},{4,12},{5,13},{6,14},{7,15},{16,24},{17,... | collective-permute-start | bytes 294920 | tf_op jit(solution)/shard_map/ppermute | solution.py:357
